TPU v7x, 256 devices: a whole 4x4x8 slice. The times are simulated.
256 devices in a mesh: slab: 128 (over y_lo, z, x, core), grp: 2 (over y_hi).
Axes of the slice: x: 4, y: 4 (y_hi: 2, y_lo: 2; y = y_hi * 2 + y_lo), z: 8, core: 2. Of those that a mesh axis runs over, the one named last changes fastest.
Arguments:
- density: float32 [512, 512, 512], P('slab', 'grp'), may hold values from -12 to 12
- shell_edges: int32 [3], replicated, may hold values from 1024 to 16384, as said below
- triangles: int32 [64, 3], replicated, may hold values from 0 to 1
Outputs:
- bispectrum: float32 [64], replicated
Inputs may be any that keep to these rules, and one draw needn't show every extreme that they name: shell_edges rises strictly, every entry is a perfect square, and the last entry equals (128)^2.
All inputs are finite; a program needn't handle non-finite values.
Results may differ from a plain program's by a relative error of at most 0.0003.
Values sent between devices are 32-bit elements; how exact they have to be, the bound alone decides.
A program may use at most 128 MiB of HBM per device.

v0:
```python
import math

import jax
import jax.numpy as jnp
from jax import lax
from jax.sharding import Mesh
from jax.sharding import PartitionSpec as P

SLAB = ("slab_0", "slab_1", "slab_2", "slab_3")
SLAB_GRP = ("slab_0", "slab_1", "slab_2", "slab_3", "grp")


def one_axis_at_a_time(x, axes):
    for axis in axes:
        x = lax.psum(x, axis)
    return x


def signed_wave(entries, length, offset):
    positions = offset + lax.iota(jnp.int32, entries)
    return jnp.where(positions < length // 2, positions, positions - length)


def phase_pair(left_count, right_count, length, exponent_sign):
    left_index = lax.iota(jnp.int32, left_count)[:, None]
    right_index = lax.iota(jnp.int32, right_count)[None, :]
    angles = 2.0 * math.pi / length * (left_index * right_index % length).astype(jnp.float32)
    return (jnp.cos(angles), exponent_sign * jnp.sin(angles))


def smallest_split(length):
    factor = 1
    for candidate in range(1, length + 1):
        if candidate * candidate > length:
            break
        if length % candidate == 0:
            factor = candidate
    return factor


def complex_product(first_real, first_imag, second_real, second_imag, formula):

    def contract(left_operand, right_operand):
        return jnp.einsum(formula, left_operand, right_operand, precision=lax.Precision.HIGHEST)

    real_out = contract(first_real, second_real) - contract(first_imag, second_imag)
    imag_out = contract(first_imag, second_real) + contract(first_real, second_imag)
    return (real_out, imag_out)


def transform_line(real_part, imag_part, position, exponent_sign):
    full_shape = real_part.shape
    length = full_shape[position]
    first_factor = smallest_split(length)
    second_factor = length // first_factor
    split_shape = full_shape[:position] + (first_factor, second_factor) + full_shape[position + 1 :]
    trailing = len(full_shape) - position - 1
    before_letters = "pqrs"[:position]
    after_letters = "tuvw"[:trailing]
    cos_first, sin_first = phase_pair(first_factor, first_factor, first_factor, exponent_sign)
    real_part, imag_part = complex_product(
        real_part.reshape(split_shape),
        imag_part.reshape(split_shape),
        cos_first,
        sin_first,
        before_letters + "ab" + after_letters + ",ak->" + before_letters + "kb" + after_letters,
    )
    cos_twist, sin_twist = phase_pair(first_factor, second_factor, length, exponent_sign)
    twist_shape = (1,) * position + (first_factor, second_factor) + (1,) * trailing
    cos_twist = cos_twist.reshape(twist_shape)
    sin_twist = sin_twist.reshape(twist_shape)
    real_part, imag_part = (
        real_part * cos_twist - imag_part * sin_twist,
        imag_part * cos_twist + real_part * sin_twist,
    )
    cos_second, sin_second = phase_pair(second_factor, second_factor, second_factor, exponent_sign)
    real_part, imag_part = complex_product(
        real_part,
        imag_part,
        cos_second,
        sin_second,
        before_letters + "kb" + after_letters + ",bm->" + before_letters + "mk" + after_letters,
    )
    return (real_part.reshape(full_shape), imag_part.reshape(full_shape))


def forward_depth(density, depth_count):
    length = density.shape[2]
    cos_table, sin_table = phase_pair(length, depth_count, length, -1.0)
    real_part = jnp.einsum("xyz,zk->xyk", density, cos_table, precision=lax.Precision.HIGHEST)
    imag_part = jnp.einsum("xyz,zk->xyk", density, sin_table, precision=lax.Precision.HIGHEST)
    return (real_part[None], imag_part[None])


def inverse_depth(real_part, imag_part, length):
    depth_count = real_part.shape[3]
    cos_table, sin_table = phase_pair(depth_count, length, length, 1.0)
    weights = jnp.where(lax.iota(jnp.int32, depth_count) == 0, 1.0, 2.0).astype(jnp.float32)[
        :, None
    ]
    cos_part = jnp.einsum(
        "bxyk,kz->bxyz", real_part, cos_table * weights, precision=lax.Precision.HIGHEST
    )
    sin_part = jnp.einsum(
        "bxyk,kz->bxyz", imag_part, sin_table * weights, precision=lax.Precision.HIGHEST
    )
    return cos_part - sin_part


def keep_rows(part, kept):
    if kept == part.shape[2]:
        return part
    half_kept = kept // 2
    return jnp.concatenate([part[:, :, :half_kept], part[:, :, part.shape[2] - half_kept :]], 2)


def widen_rows(part, length):
    kept = part.shape[2]
    if kept == length:
        return part
    half_kept = kept // 2
    zeros_shape = part.shape[:2] + (length - kept,) + part.shape[3:]
    return jnp.concatenate(
        [part[:, :, :half_kept], jnp.zeros(zeros_shape, part.dtype), part[:, :, half_kept:]], 2
    )


def along_columns(pieces):
    return transform_line(pieces[0], pieces[1], 1, -1.0)


def shards(density, shell_edges, triangles):
    length = density.shape[2]
    depth_count = length // 4
    slab_count = lax.axis_size(SLAB)
    kept = length // 2 if length // 2 % slab_count == 0 else length
    real_part, imag_part = forward_depth(density, depth_count)
    pieces = (
        lax.all_to_all(real_part, "grp", split_axis=3, concat_axis=2, tiled=True),
        lax.all_to_all(imag_part, "grp", split_axis=3, concat_axis=2, tiled=True),
    )
    row_real, row_imag = transform_line(pieces[0], pieces[1], 2, -1.0)
    real_part = keep_rows(row_real, kept)
    imag_part = keep_rows(row_imag, kept)
    real_part, imag_part = along_columns(
        (
            lax.all_to_all(real_part, SLAB, split_axis=2, concat_axis=1, tiled=True),
            lax.all_to_all(imag_part, SLAB, split_axis=2, concat_axis=1, tiled=True),
        )
    )
    block_rows = real_part.shape[2]
    block_depth = real_part.shape[3]
    wave_first = signed_wave(length, length, 0)
    wave_second = signed_wave(block_rows, kept, lax.axis_index(SLAB) * block_rows)
    wave_third = lax.axis_index("grp") * block_depth + lax.iota(jnp.int32, block_depth)
    squared = (
        wave_first[:, None, None] * wave_first[:, None, None]
        + wave_second[None, :, None] * wave_second[None, :, None]
        + wave_third[None, None, :] * wave_third[None, None, :]
    )
    radius = jnp.sqrt(shell_edges.astype(jnp.float32))
    volume = 4.0 * math.pi / 3.0 * (radius[1:] ** 3 - radius[:-1] ** 3)
    scales = lax.rsqrt(float(length) ** 3 * volume)
    shell_count = volume.shape[0]
    batch_size = 2

    def back_depth(pieces):
        return inverse_depth(pieces[0], pieces[1], length)

    fields = []
    for first_shell in range(0, shell_count, batch_size):
        last_shell = min(first_shell + batch_size, shell_count)
        lower_edge = shell_edges[first_shell:last_shell][:, None, None, None]
        upper_edge = shell_edges[first_shell + 1 : last_shell + 1][:, None, None, None]
        inside = (squared[None] >= lower_edge) & (squared[None] < upper_edge)
        weight = jnp.where(inside, scales[first_shell:last_shell][:, None, None, None], 0.0)
        shell_real, shell_imag = transform_line(real_part * weight, imag_part * weight, 1, 1.0)
        shell_real, shell_imag = transform_line(
            widen_rows(
                lax.all_to_all(shell_real, SLAB, split_axis=1, concat_axis=2, tiled=True), length
            ),
            widen_rows(
                lax.all_to_all(shell_imag, SLAB, split_axis=1, concat_axis=2, tiled=True), length
            ),
            2,
            1.0,
        )
        fields.append(
            back_depth(
                (
                    lax.all_to_all(shell_real, "grp", split_axis=2, concat_axis=3, tiled=True),
                    lax.all_to_all(shell_imag, "grp", split_axis=2, concat_axis=3, tiled=True),
                )
            )
        )
    stacked = jnp.concatenate(fields, 0).reshape(shell_count, -1)
    partial_cube = jnp.stack(
        [
            jnp.einsum(
                "jc,mc->jm",
                stacked[shell_index][None, :] * stacked,
                stacked,
                precision=lax.Precision.HIGHEST,
            )
            for shell_index in range(shell_count)
        ]
    )
    triple_cube = one_axis_at_a_time(partial_cube, SLAB_GRP)
    shell_norms = volume ** (1.0 / 6.0)
    scaled = (
        triple_cube
        * shell_norms[:, None, None]
        * shell_norms[None, :, None]
        * shell_norms[None, None, :]
        / float(length) ** 3
    )
    shells = lax.iota(jnp.int32, shell_count)[None, :]
    pick_first = (triangles[:, 0:1] == shells).astype(jnp.float32)
    pick_second = (triangles[:, 1:2] == shells).astype(jnp.float32)
    pick_third = (triangles[:, 2:3] == shells).astype(jnp.float32)
    return jnp.einsum(
        "ti,tj,tm,ijm->t",
        pick_first,
        pick_second,
        pick_third,
        scaled,
        precision=lax.Precision.HIGHEST,
    )


def solution(mesh):
    torus = Mesh(
        mesh.devices.reshape(2, 8, 4, 2, mesh.shape["grp"]),
        ("slab_0", "slab_1", "slab_2", "slab_3", "grp"),
    )
    return jax.shard_map(
        shards,
        mesh=torus,
        in_specs=(P(SLAB, "grp", None), P(), P()),
        out_specs=P(),
        check_vma=False,
    )
```

profile of v0, /device:TPU:1, one launch (start us, length us, event | category | flops | bytes accessed | tf_op | source)
XLA Modules:
  0.0 376.3 jit_solution(8907699115682501809)
XLA Ops:
  0.0 1.6 copy-done
  1.6 3.2 convolution_bitcast_fusion
  5.9 5.1 %all-to-all-start.1 = ((f32[1,4,256,128]{2,1,0,3:T(4,128)}), f32[1,4,256,128]{2,1,0,3:T(4,128)S(1)}, u32[]{:S(2)}, u32[]{:S(2)}) async-start(f32[1,4,256,128]{2,1,0,3:T(4,128)} %copy.144), calls=%async_computation.1 | async-start | bytes 1048576 | tf_op jit(solution)/shard_map/all_to_all | solution.py:140
  11.1 3.2 convolution_bitcast_fusion.1
  15.8 3.1 all-to-all-done.1
  18.9 3.7 all-to-all-start
  23.1 1.5 fusion.64
  24.6 4.9 %all-to-all-done = f32[1,4,256,128]{2,1,0,3:T(4,128)S(1)} async-done(((f32[1,4,256,128]{2,1,0,3:T(4,128)}), f32[1,4,256,128]{2,1,0,3:T(4,128)S(1)}, u32[]{:S(2)}, u32[]{:S(2)}) %all-to-all-start) | async-done | bytes 524320 | tf_op jit(solution)/shard_map/all_to_all | solution.py:139
  30.4 1.4 copy.142
  31.8 1.5 fusion.68
  33.3 1.5 fusion.36
  34.9 1.8 subtract_bitcast_fusion.3
  41.6 1.6 reshape.376
  43.2 17.0 %all-to-all-start.2 = ((f32[128,1,512]{2,1,0:T(1,128)}), f32[128,1,512]{2,1,0:T(1,128)S(1)}, u32[]{:S(2)}, u32[]{:S(2)}) async-start(f32[128,1,512]{2,1,0:T(1,128)} %reshape.376), calls=%async_computation.2 | async-start | bytes 524288 | tf_op jit(solution)/shard_map/all_to_all | solution.py:147
  63.7 11.6 %all-to-all-done.2 = f32[128,1,512]{2,1,0:T(1,128)S(1)} async-done(((f32[128,1,512]{2,1,0:T(1,128)}), f32[128,1,512]{2,1,0:T(1,128)S(1)}, u32[]{:S(2)}, u32[]{:S(2)}) %all-to-all-start.2) | async-done | bytes 262176 | tf_op jit(solution)/shard_map/all_to_all | solution.py:147
  75.3 5.7 %all-to-all-start.3 = ((f32[128,1,512]{2,1,0:T(1,128)}), f32[128,1,512]{2,1,0:T(1,128)S(1)}, u32[]{:S(2)}, u32[]{:S(2)}) async-start(f32[128,1,512]{2,1,0:T(1,128)} %reshape.374), calls=%async_computation.3 | async-start | bytes 524288 | tf_op jit(solution)/shard_map/all_to_all | solution.py:148
  83.7 12.4 %all-to-all-done.3 = f32[128,1,512]{2,1,0:T(1,128)S(1)} async-done(((f32[128,1,512]{2,1,0:T(1,128)}), f32[128,1,512]{2,1,0:T(1,128)S(1)}, u32[]{:S(2)}, u32[]{:S(2)}) %all-to-all-start.3) | async-done | bytes 262176 | tf_op jit(solution)/shard_map/all_to_all | solution.py:148
  107.2 1.3 fusion.39
  109.6 1.4 subtract_bitcast_fusion.2
  111.0 1.6 fusion.52
  112.6 1.6 fusion.32
  114.8 1.8 copy.321
  116.6 3.1 reshape.378
  119.7 7.2 %all-to-all-start.5 = ((f32[128,1,1024]{2,1,0:T(1,128)}), f32[128,1,1024]{2,1,0:T(1,128)}, u32[]{:S(2)}, u32[]{:S(2)}) async-start(f32[128,1,1024]{2,1,0:T(1,128)} %reshape.378), calls=%async_computation.5 | async-start | bytes 1048576 | tf_op jit(solution)/shard_map/all_to_all | solution.py:183
  126.9 1.6 fusion.56
  128.5 1.6 fusion.33
  131.6 1.9 reshape.380
  133.5 13.5 %all-to-all-done.5 = f32[128,1,1024]{2,1,0:T(1,128)} async-done(((f32[128,1,1024]{2,1,0:T(1,128)}), f32[128,1,1024]{2,1,0:T(1,128)}, u32[]{:S(2)}, u32[]{:S(2)}) %all-to-all-start.5) | async-done | bytes 524320 | tf_op jit(solution)/shard_map/all_to_all | solution.py:183
  147.0 5.6 %all-to-all-start.4 = ((f32[128,1,1024]{2,1,0:T(1,128)}), f32[128,1,1024]{2,1,0:T(1,128)S(1)}, u32[]{:S(2)}, u32[]{:S(2)}) async-start(f32[128,1,1024]{2,1,0:T(1,128)} %reshape.380), calls=%async_computation.4 | async-start | bytes 1048576 | tf_op jit(solution)/shard_map/all_to_all | solution.py:180
  152.6 2.9 reduce.5
  158.1 15.0 %all-to-all-done.4 = f32[128,1,1024]{2,1,0:T(1,128)S(1)} async-done(((f32[128,1,1024]{2,1,0:T(1,128)}), f32[128,1,1024]{2,1,0:T(1,128)S(1)}, u32[]{:S(2)}, u32[]{:S(2)}) %all-to-all-start.4) | async-done | bytes 524320 | tf_op jit(solution)/shard_map/all_to_all | solution.py:180
  173.1 1.9 reduce.4
  177.2 2.9 fusion.16
  180.1 2.9 fusion.14
  183.0 3.1 fusion.22
  186.1 3.5 subtract_bitcast_fusion.1
  189.6 2.3 fusion.6
  192.0 2.4 add_bitcast_fusion
  194.4 1.6 copy.196
  196.0 2.7 copy.319
  198.7 4.0 %reshape.384 = f32[2,1,131072]{2,1,0:T(1,128)} reshape(f32[512,2,4,64]{3,2,1,0:T(4,128)} %bitcast.266) | data formatting | bytes 2097152
  202.7 3.6 all-to-all-start.7
  206.3 3.9 %fusion.8 = f32[32,2,4,16,64]{4,0,3,2,1:T(8,128)S(1)} fusion(f32[2,4,16,32,64]{4,2,3,1,0:T(8,128)} %copy-done.2), kind=kOutput, calls=%fused_computation.19 | convolution fusion | flops 100677632 | bytes 2097152 | tf_op jit(solution)/shard_map/pqkbt,bm->pqmkt/dot_general | solution.py:44
  210.2 2.3 subtract_bitcast_fusion
  213.7 2.7 copy.320
  216.4 4.0 %reshape.382 = f32[2,1,131072]{2,1,0:T(1,128)} reshape(f32[512,2,4,64]{3,2,1,0:T(4,128)} %bitcast.268) | data formatting | bytes 2097152
  221.1 4.6 %all-to-all-start.6 = ((f32[2,1,131072]{2,1,0:T(1,128)}), f32[2,1,131072]{2,1,0:T(1,128)}, u32[]{:S(2)}, u32[]{:S(2)}) async-start(f32[2,1,131072]{2,1,0:T(1,128)} %reshape.382), calls=%async_computation.6 | async-start | bytes 2097152 | tf_op jit(solution)/shard_map/all_to_all | solution.py:191
  225.7 4.9 %reduce.7 = f32[2,131072]{1,0:T(2,128)S(1)} reduce(f32[2,1,131072]{2,1,0:T(1,128)} %copy-done.4, f32[]{:T(128)} %broadcast.686), dimensions={1}, to_apply=%all_to_all.120.reduce_sub_computation | reduce | bytes 2097156 | tf_op jit(solution)/shard_map/all_to_all | solution.py:192
  230.7 1.7 reshape.385
  232.4 1.3 copy.226
  234.8 5.0 %all-to-all-done.6 = f32[2,1,131072]{2,1,0:T(1,128)} async-done(((f32[2,1,131072]{2,1,0:T(1,128)}), f32[2,1,131072]{2,1,0:T(1,128)}, u32[]{:S(2)}, u32[]{:S(2)}) %all-to-all-start.6) | async-done | bytes 1048608 | tf_op jit(solution)/shard_map/all_to_all | solution.py:191
  239.8 4.9 %reduce.6 = f32[2,131072]{1,0:T(2,128)S(1)} reduce(f32[2,1,131072]{2,1,0:T(1,128)} %all-to-all-done.6, f32[]{:T(128)} %broadcast.686), dimensions={1}, to_apply=%all_to_all.116.reduce_sub_computation | reduce | bytes 2097156 | tf_op jit(solution)/shard_map/all_to_all | solution.py:191
  244.7 1.7 reshape.383
  246.4 1.5 copy.225
  248.1 4.6 %fusion.101 = f32[2,4,256,512]{3,2,1,0:T(8,128)S(1)} fusion(f32[2,4,256,128]{2,3,1,0:T(8,128)S(1)} %bitcast.258, f32[128]{0:T(128)S(1)} %compare_select_fusion.2), kind=kOutput, calls=%fused_computation.128 | convolution fusion | flops 1611595776 | bytes 5243392 | tf_op jit(solution)/shard_map/bxyk,kz->bxyz/dot_general | solution.py:101
  252.7 4.7 %convolution_subtract_fusion = f32[2,4,256,512]{3,2,1,0:T(8,128)S(1)} fusion(f32[2,4,256,512]{3,2,1,0:T(8,128)S(1)} %fusion.101, f32[2,4,256,128]{2,3,1,0:T(8,128)S(1)} %bitcast.273, f32[128]{0:T(128)S(1)} %compare_select_fusion.2), kind=kOutput, calls=%fused_computation.6 | convolution fusion | flops 1612644352 | bytes 9437696 | tf_op jit(solution)/shard_map/bxyk,kz->bxyz/dot_general | solution.py:104
  257.8 1.3 broadcast_multiply_fusion.1
  259.1 39.1 %fusion.40 = f32[1,2,2]{2,1,0:T(2,128)S(1)} fusion(f32[2,4,256,512]{3,2,1,0:T(8,128)S(1)} %convolution_subtract_fusion, f32[2,4,256,512]{3,2,1,0:T(8,128)S(1)} %get-tuple-element.9), kind=kOutput, calls=%fused_computation.59 | convolution fusion | flops 25165824 | bytes 8388624 | tf_op jit(solution)/shard_map/jc,mc->jm/dot_general | solution.py:199
  298.2 39.1 %fusion.45 = f32[1,2,2]{2,1,0:T(2,128)S(1)} fusion(f32[2,4,256,512]{3,2,1,0:T(8,128)S(1)} %convolution_subtract_fusion, f32[2,4,256,512]{3,2,1,0:T(8,128)S(1)} %get-tuple-element.10), kind=kOutput, calls=%fused_computation.60 | convolution fusion | flops 25165824 | bytes 8388624 | tf_op jit(solution)/shard_map/jc,mc->jm/dot_general | solution.py:199
  337.4 3.8 %psum.35 = f32[2,2,2]{2,1,0:T(2,128)S(1)} all-reduce(f32[2,2,2]{2,1,0:T(2,128)S(1)} %pad_maximum_fusion.4), channel_id=1, replica_groups=mesh['slab_0'=2,'slab_1'=8,'slab_2'=4,'slab_3'=2,'grp'=2] {'slab_0'}, use_global_device_ids=true, to_apply=%region_0.1 | all-reduce | flops 8 | bytes 64 | tf_op jit(solution)/shard_map/psum | solution.py:15
  341.2 11.9 %psum.36 = f32[2,2,2]{2,1,0:T(2,128)S(1)} all-reduce(f32[2,2,2]{2,1,0:T(2,128)S(1)} %psum.35), channel_id=1, replica_groups=mesh['slab_0'=2,'slab_1'=8,'slab_2'=4,'slab_3'=2,'grp'=2] {'slab_1'}, use_global_device_ids=true, to_apply=%region_1.2 | all-reduce | flops 8 | bytes 64 | tf_op jit(solution)/shard_map/psum | solution.py:15
  353.2 6.0 %psum.37 = f32[2,2,2]{2,1,0:T(2,128)S(1)} all-reduce(f32[2,2,2]{2,1,0:T(2,128)S(1)} %psum.36), channel_id=1, replica_groups=mesh['slab_0'=2,'slab_1'=8,'slab_2'=4,'slab_3'=2,'grp'=2] {'slab_2'}, use_global_device_ids=true, to_apply=%region_2.3 | all-reduce | flops 8 | bytes 64 | tf_op jit(solution)/shard_map/psum | solution.py:15
  359.2 10.5 %psum.38 = f32[2,2,2]{2,1,0:T(2,128)S(1)} all-reduce(f32[2,2,2]{2,1,0:T(2,128)S(1)} %psum.37), channel_id=1, replica_groups=mesh['slab_0'=2,'slab_1'=8,'slab_2'=4,'slab_3'=2,'grp'=2] {'slab_3'}, use_global_device_ids=true, to_apply=%region_3.4 | all-reduce | flops 8 | bytes 64 | tf_op jit(solution)/shard_map/psum | solution.py:15
  369.8 5.3 %psum.39 = f32[2,2,2]{2,1,0:T(2,128)S(1)} all-reduce(f32[2,2,2]{2,1,0:T(2,128)S(1)} %psum.38), channel_id=1, replica_groups=mesh['slab_0'=2,'slab_1'=8,'slab_2'=4,'slab_3'=2,'grp'=2] {'grp'}, use_global_device_ids=true, to_apply=%region_4.5 | all-reduce | flops 8 | bytes 64 | tf_op jit(solution)/shard_map/psum | solution.py:15
  (91 shorter events, 38.4 us)
Async XLA Ops:
  0.0 1.6 copy-start
  5.9 8.4 %copy-start.6 = (s32[3]{0:T(128)S(1)}, s32[3]{0:T(128)}, u32[]{:S(2)}) copy-start(s32[3]{0:T(128)} %param.4) | copy-start | bytes 40
  5.9 13.0 %all-to-all-start.1 = ((f32[1,4,256,128]{2,1,0,3:T(4,128)}), f32[1,4,256,128]{2,1,0,3:T(4,128)S(1)}, u32[]{:S(2)}, u32[]{:S(2)}) async-start(f32[1,4,256,128]{2,1,0,3:T(4,128)} %copy.144), calls=%async_computation.1 | async-start | bytes 1048576 | tf_op jit(solution)/shard_map/all_to_all | solution.py:140
  18.9 10.6 %all-to-all-start = ((f32[1,4,256,128]{2,1,0,3:T(4,128)}), f32[1,4,256,128]{2,1,0,3:T(4,128)S(1)}, u32[]{:S(2)}, u32[]{:S(2)}) async-start(f32[1,4,256,128]{2,1,0,3:T(4,128)} %copy.140), calls=%async_computation | async-start | bytes 1048576 | tf_op jit(solution)/shard_map/all_to_all | solution.py:139
  43.2 32.1 %all-to-all-start.2 = ((f32[128,1,512]{2,1,0:T(1,128)}), f32[128,1,512]{2,1,0:T(1,128)S(1)}, u32[]{:S(2)}, u32[]{:S(2)}) async-start(f32[128,1,512]{2,1,0:T(1,128)} %reshape.376), calls=%async_computation.2 | async-start | bytes 524288 | tf_op jit(solution)/shard_map/all_to_all | solution.py:147
  75.3 20.8 %all-to-all-start.3 = ((f32[128,1,512]{2,1,0:T(1,128)}), f32[128,1,512]{2,1,0:T(1,128)S(1)}, u32[]{:S(2)}, u32[]{:S(2)}) async-start(f32[128,1,512]{2,1,0:T(1,128)} %reshape.374), calls=%async_computation.3 | async-start | bytes 524288 | tf_op jit(solution)/shard_map/all_to_all | solution.py:148
  119.7 27.2 %all-to-all-start.5 = ((f32[128,1,1024]{2,1,0:T(1,128)}), f32[128,1,1024]{2,1,0:T(1,128)}, u32[]{:S(2)}, u32[]{:S(2)}) async-start(f32[128,1,1024]{2,1,0:T(1,128)} %reshape.378), calls=%async_computation.5 | async-start | bytes 1048576 | tf_op jit(solution)/shard_map/all_to_all | solution.py:183
  147.0 26.1 %all-to-all-start.4 = ((f32[128,1,1024]{2,1,0:T(1,128)}), f32[128,1,1024]{2,1,0:T(1,128)S(1)}, u32[]{:S(2)}, u32[]{:S(2)}) async-start(f32[128,1,1024]{2,1,0:T(1,128)} %reshape.380), calls=%async_computation.4 | async-start | bytes 1048576 | tf_op jit(solution)/shard_map/all_to_all | solution.py:180
  175.7 1.0 copy-start.5
  189.6 2.3 copy-start.2
  202.7 18.4 %all-to-all-start.7 = ((f32[2,1,131072]{2,1,0:T(1,128)}), f32[2,1,131072]{2,1,0:T(1,128)S(1)}, u32[]{:S(2)}, u32[]{:S(2)}) async-start(f32[2,1,131072]{2,1,0:T(1,128)} %reshape.384), calls=%async_computation.7 | async-start | bytes 2097152 | tf_op jit(solution)/shard_map/all_to_all | solution.py:192
  221.1 4.6 %copy-start.4 = (f32[2,1,131072]{2,1,0:T(1,128)}, f32[2,1,131072]{2,1,0:T(1,128)S(1)}, u32[]{:S(2)}) copy-start(f32[2,1,131072]{2,1,0:T(1,128)S(1)} %all-to-all-done.7) | copy-start | bytes 3145732
  221.1 18.7 %all-to-all-start.6 = ((f32[2,1,131072]{2,1,0:T(1,128)}), f32[2,1,131072]{2,1,0:T(1,128)}, u32[]{:S(2)}, u32[]{:S(2)}) async-start(f32[2,1,131072]{2,1,0:T(1,128)} %reshape.382), calls=%async_computation.6 | async-start | bytes 2097152 | tf_op jit(solution)/shard_map/all_to_all | solution.py:191
  248.1 4.6 %copy-start.3 = (f32[2,4,256,2,64]{2,4,3,1,0:T(8,128)S(1)}, f32[2,4,256,2,64]{2,4,3,1,0:T(8,128)}, u32[]{:S(2)}) copy-start(f32[2,4,256,2,64]{2,4,3,1,0:T(8,128)} %copy.199) | copy-start | bytes 3145732
  298.2 42.9 %copy-start.7 = (s32[64,3]{0,1:T(4,128)S(1)}, s32[64,3]{0,1:T(4,128)}, u32[]{:S(2)}) copy-start(s32[64,3]{0,1:T(4,128)} %param.5) | copy-start | bytes 2308
  298.2 77.6 %copy-start.1 = (f32[4,256,512]{2,1,0:T(8,128)S(1)}, f32[4,256,512]{2,1,0:T(8,128)}, u32[]{:S(2)}) copy-start(f32[4,256,512]{2,1,0:T(8,128)} %param.3) | copy-start | bytes 6291460
where the time goes:
time: 383 us; the launch traced here: 376 us
  matrix products  148 us (39%)
  waiting for transfers between devices  66.1 us (17%)
  starting transfers between devices  52.5 us (14%)
  local copies, waits for them, and re-layouts  51.2 us (13%)
  blocking collectives  37.5 us (10%)
  other arithmetic  19.9 us (5%)
    dot_general x2, matrix products, shards(): jnp.einsum('jc,mc->jm', stacked[shell_index][None, :] * stacked, stacked,...  78.3 us
    dot_general x32, matrix products, contract(): jnp.einsum(formula, left_operand, right_operand, precision=lax.Precision....  53.2 us
    psum x5, blocking collectives, one_axis_at_a_time(): x = lax.psum(x, axis)  37.5 us
    unnamed x29, local copies, waits for them, and re-layouts  23.6 us
    all_to_all x1, starting transfers between devices, shards(): lax.all_to_all(real_part, SLAB, split_axis=2, concat_axis=1, tiled=True)  17 us
    all_to_all x1, waiting for transfers between devices, shards(): lax.all_to_all(shell_real, SLAB, split_axis=1, concat_axis=2, tiled=True)  15 us
    all_to_all x1, waiting for transfers between devices, shards(): lax.all_to_all(shell_imag, SLAB, split_axis=1, concat_axis=2, tiled=True)  13.5 us
    all_to_all x1, waiting for transfers between devices, shards(): lax.all_to_all(imag_part, SLAB, split_axis=2, concat_axis=1, tiled=True)  12.4 us
  transfers between devices with their start and end apart: 8, of which 8 were waited for; matrix products, arithmetic and copies ran while one was open for 13% of the time, Pallas kernels for 0%

commit v1 on v0

v1 whole, which is shorter than its diff:
```python
import math

import jax
import jax.numpy as jnp
import numpy as np
from jax import lax
from jax.experimental import pallas as pl
from jax.experimental.pallas import tpu as pltpu
from jax.sharding import PartitionSpec as P

MESH = pl.DeviceIdType.MESH
LANES = 128
SUB = 8
STEP = 37


def halves(table):
    table = np.asarray(table, np.float32)
    high = table.astype(jnp.bfloat16)
    low = (table - high.astype(np.float32)).astype(jnp.bfloat16)
    return np.stack([high, low])


def tables(length, kept, coarse):
    depth = kept // 2
    line = np.arange(length)
    wave = np.arange(kept)
    wave = np.where(wave < depth, wave, wave - kept)
    deep = np.arange(depth)
    points = np.arange(coarse)

    def angle(left, right, period):
        return 2.0 * np.pi / period * (left[:, None] * right[None, :] % period)

    a = angle(line, deep, length)
    depth_in = np.concatenate([np.cos(a), -np.sin(a)], 1)
    a = angle(wave, line, length)
    forward = np.stack([np.cos(a), np.sin(a)])
    a = angle(np.concatenate([line[0::2], line[1::2]]), wave, length)
    inverse = np.stack([np.cos(a), np.sin(a)])
    a = angle(points, wave, coarse)
    rows_out = np.stack([np.cos(a), np.sin(a)])
    a = angle(deep, points, coarse)
    weight = np.where(deep == 0, 1.0, 2.0)[:, None]
    depth_out = np.concatenate([weight * np.cos(a), -weight * np.sin(a)], 0)
    return [halves(t) for t in (depth_in, forward, inverse, rows_out, depth_out)]


def split(x):
    high = x.astype(jnp.bfloat16)
    return high, (x - high.astype(jnp.float32)).astype(jnp.bfloat16)


def dot(left, right):
    def part(i, j):
        return jnp.dot(left[i], right[j], preferred_element_type=jnp.float32)

    return part(0, 0) + (part(0, 1) + part(1, 0))


def both(ref, index, columns=slice(None)):
    return ref[0, index, :, columns], ref[1, index, :, columns]


def kernel(
    slab_count, edges, x_ref, depth_in, forward, inverse_hbm, rows_hbm, depth_hbm,
    out_ref,
    inverse, rows_out, depth_out, send1, recv1, send2, recv2, send3, recv3, load_sems, send_sems, recv_sems,
):
    devices = 2 * slab_count
    slab, grp = lax.axis_index("slab"), lax.axis_index("grp")
    me = grp * slab_count + slab
    length = x_ref.shape[2]

    def partner(t):
        other = lax.rem(me + t * STEP, devices)
        return other, (lax.rem(other, slab_count), lax.div(other, slab_count))

    barrier = pltpu.get_barrier_semaphore()

    def greet(t, carry):
        pl.semaphore_signal(barrier, inc=1, device_id=partner(t)[1], device_id_type=MESH)
        return carry

    lax.fori_loop(1, devices, greet, 0)
    loads = [
        pltpu.make_async_copy(source, target, load_sems.at[n])
        for n, (source, target) in enumerate(
            ((inverse_hbm, inverse), (rows_hbm, rows_out), (depth_hbm, depth_out))
        )
    ]
    for load in loads:
        load.start()

    def tile(index):
        return pl.ds(pl.multiple_of(index * SUB, SUB), SUB)

    def exchange(send, recv, n):
        pltpu.make_async_copy(send.at[tile(me)], recv.at[tile(me)], recv_sems.at[n]).start()

        def push(t, carry):
            other, where = partner(t)
            pltpu.make_async_remote_copy(
                src_ref=send.at[tile(other)],
                dst_ref=recv.at[tile(me)],
                send_sem=send_sems.at[n],
                recv_sem=recv_sems.at[n],
                device_id=where,
                device_id_type=MESH,
            ).start()
            return carry

        lax.fori_loop(1, devices, push, 0)
        pltpu.make_async_copy(recv, recv, recv_sems.at[n]).wait()

    def sent(send, n):
        part = send.at[pl.ds(0, (devices - 1) * SUB)]
        pltpu.make_async_copy(part, part, send_sems.at[n]).wait()

    half = x_ref.shape[1]
    kept = forward.shape[2]
    table_in = (depth_in[0], depth_in[1])
    cosine, sine = both(forward, 0, slice(0, half)), both(forward, 1, slice(0, half))
    for i in range(x_ref.shape[0]):
        modes = split(dot(split(x_ref[i]), table_in))
        c, s = dot(cosine, modes), dot(sine, modes)
        send1[pl.ds(2 * i, kept, stride=SUB), :] = c[:, :LANES] + s[:, LANES:]
        send1[pl.ds(2 * i + 1, kept, stride=SUB), :] = c[:, LANES:] - s[:, :LANES]

    pl.semaphore_wait(barrier, devices - 1)
    exchange(send1, recv1, 0)

    sign = (1 - 2 * lax.rem(me, 2)).astype(jnp.float32)

    def joined(part):
        first = recv1[pl.ds(part, length, stride=2), :]
        second = recv1[pl.ds(slab_count * SUB + part, length, stride=2), :]
        return first + sign * second

    line = split(jnp.concatenate([joined(0), joined(1)], 1))
    c, s = dot(both(forward, 0), line), dot(both(forward, 1), line)
    real, imag = c[:, :LANES] + s[:, LANES:], c[:, LANES:] - s[:, :LANES]
    row = lax.broadcasted_iota(jnp.int32, real.shape, 0)
    first = jnp.where(row < kept // 2, row, row - kept)
    second = jnp.where(me < kept // 2, me, me - kept)
    third = lax.broadcasted_iota(jnp.int32, real.shape, 1)
    squared = first * first + second * second + third * third
    radius = [jnp.sqrt(jnp.full((1, LANES), edges[n], jnp.int32).astype(jnp.float32)) for n in range(3)]
    pieces = []
    for n in range(2):
        inner, outer = radius[n], radius[n + 1]
        volume = 4.0 * math.pi / 3.0 * (outer * outer * outer - inner * inner * inner)
        scale = lax.rsqrt(float(length) ** 3 * volume)
        inside = (squared >= edges[n]) & (squared < edges[n + 1])
        weight = jnp.where(inside, jnp.broadcast_to(scale, real.shape), 0.0)
        pieces += [real * weight, imag * weight]
    shells = split(jnp.concatenate(pieces, 1))
    loads[0].wait()
    c, s = dot(both(inverse, 0), shells), dot(both(inverse, 1), shells)
    for n in range(2):
        re, im = slice(2 * n * LANES, (2 * n + 1) * LANES), slice((2 * n + 1) * LANES, (2 * n + 2) * LANES)
        back_real, back_imag = c[:, re] - s[:, im], c[:, im] + s[:, re]
        for i in range(2):
            rows = slice(i * devices, (i + 1) * devices)
            send2[pl.ds(4 * n + i, devices, stride=SUB), :] = back_real[rows]
            send2[pl.ds(4 * n + 2 + i, devices, stride=SUB), :] = back_imag[rows]
    exchange(send2, recv2, 1)

    loads[1].wait()
    loads[2].wait()
    cosine, sine = both(rows_out, 0), both(rows_out, 1)
    table_out = (depth_out[0], depth_out[1])
    totals = [0.0] * 4
    for i in range(2):
        fields = []
        for n in range(2):
            plane = split(
                jnp.concatenate(
                    [recv2[pl.ds(4 * n + i, kept, stride=SUB), :], recv2[pl.ds(4 * n + 2 + i, kept, stride=SUB), :]], 1
                )
            )
            c, s = dot(cosine, plane), dot(sine, plane)
            lines = jnp.concatenate([c[:, :LANES] - s[:, LANES:], c[:, LANES:] + s[:, :LANES]], 1)
            fields.append(dot(split(lines), table_out))
        f, g = fields
        ff, gg = f * f, g * g
        for n, product in enumerate((ff * f, ff * g, gg * f, gg * g)):
            folded = jnp.sum(product.reshape(-1, SUB, product.shape[1]), 0)
            totals[n] = totals[n] + sum(folded[:, k : k + LANES] for k in range(0, product.shape[1], LANES))
    lane = lax.broadcasted_iota(jnp.int32, (1, LANES), 1)
    packed = jnp.zeros((1, LANES), jnp.float32)
    for n in range(4):
        packed = jnp.where(lane == n, jnp.sum(totals[n], keepdims=True), packed)
    send3[0] = packed

    pltpu.make_async_copy(send3, recv3.at[pl.ds(me, 1)], recv_sems.at[2]).start()

    def tell(t, carry):
        pltpu.make_async_remote_copy(
            src_ref=send3,
            dst_ref=recv3.at[pl.ds(me, 1)],
            send_sem=send_sems.at[2],
            recv_sem=recv_sems.at[2],
            device_id=partner(t)[1],
            device_id_type=MESH,
        ).start()
        return carry

    lax.fori_loop(1, devices, tell, 0)
    pltpu.make_async_copy(recv3, recv3, recv_sems.at[2]).wait()
    out_ref[...] = jnp.sum(recv3[...], 0)
    sent(send1, 0)
    sent(send2, 1)
    part = recv3.at[pl.ds(0, devices - 1)]
    pltpu.make_async_copy(part, part, send_sems.at[2]).wait()


def shards(density, shell_edges, triangles):
    planes, half, length = density.shape
    slab_count = lax.axis_size("slab")
    devices = 2 * slab_count
    kept, coarse = length // 2, 3 * length // 4
    depth_in, forward, inverse, rows_out, depth_out = tables(length, kept, coarse)
    vmem = pl.BlockSpec(memory_space=pltpu.VMEM)
    hbm = pl.BlockSpec(memory_space=pl.ANY)
    block = pltpu.VMEM((devices * SUB, LANES), jnp.float32)
    sums = pl.pallas_call(
        lambda *refs: kernel(slab_count, *refs),
        out_shape=jax.ShapeDtypeStruct((1, LANES), jnp.float32),
        in_specs=[pl.BlockSpec(memory_space=pltpu.SMEM), vmem, vmem, vmem, hbm, hbm, hbm],
        out_specs=vmem,
        scratch_shapes=[
            pltpu.VMEM(inverse.shape, jnp.bfloat16),
            pltpu.VMEM(rows_out.shape, jnp.bfloat16),
            pltpu.VMEM(depth_out.shape, jnp.bfloat16),
            block, block, block, block,
            pltpu.VMEM((1, 1, LANES), jnp.float32),
            pltpu.VMEM((devices, 1, LANES), jnp.float32),
            pltpu.SemaphoreType.DMA((3,)),
            pltpu.SemaphoreType.DMA((3,)),
            pltpu.SemaphoreType.DMA((3,)),
        ],
        compiler_params=pltpu.CompilerParams(
            collective_id=0, has_side_effects=True, vmem_limit_bytes=60 << 20
        ),
    )(shell_edges, density, depth_in, forward, inverse, rows_out, depth_out)
    radius = jnp.sqrt(shell_edges.astype(jnp.float32))
    volume = 4.0 * math.pi / 3.0 * (radius[1:] ** 3 - radius[:-1] ** 3)
    norms = volume ** (1.0 / 6.0)
    finer = (float(length) / float(coarse)) ** 2 / float(length) ** 3
    ones = jnp.sum(triangles, 1)
    out = jnp.zeros(ones.shape, jnp.float32)
    for n in range(4):
        out = jnp.where(ones == n, sums[0, n] * norms[0] ** (3 - n) * norms[1] ** n * finer, out)
    return out


def solution(mesh):
    return jax.shard_map(
        shards,
        mesh=mesh,
        in_specs=(P("slab", "grp", None), P(), P()),
        out_specs=P(),
        check_vma=False,
    )
```

time: 383 us -> 100 us (0.26); the launches traced: 376 us -> 100 us
  matrix products: 148 us -> 0 us
  Pallas kernels: 0 us -> 89.5 us
  waiting for transfers between devices: 66.1 us -> 0 us
  starting transfers between devices: 52.5 us -> 0 us
  local copies, waits for them, and re-layouts: 51.2 us -> 1.98 us
  blocking collectives: 37.5 us -> 0 us
  other arithmetic: 19.9 us -> 1.28 us
  between operations: 1.31 us -> 7.27 us
    dot_general x39 -> x0, matrix products: 148 us -> none  [the longest x2 78.3 us: shards(): jnp.einsum('jc,mc->jm', stacked[shell_index][None, :] * stacked, stacked,...]
    pallas_call x0 -> x1, Pallas kernels: none -> 89.5 us  [shards(): pl.pallas_call(lambda *refs: kernel(slab_count, *refs), out_shape=jax.Sha...]
    all_to_all x8 -> x0, waiting for transfers between devices: 66.1 us -> none  [the longest x1 15 us: shards(): lax.all_to_all(shell_real, SLAB, split_axis=1, concat_axis=2, tiled=True)]
    all_to_all x8 -> x0, starting transfers between devices: 52.5 us -> none  [the longest x1 17 us: shards(): lax.all_to_all(real_part, SLAB, split_axis=2, concat_axis=1, tiled=True)]
    psum x5 -> x0, blocking collectives: 37.5 us -> none  [one_axis_at_a_time(): x = lax.psum(x, axis)]
    unnamed x29 -> x2, local copies, waits for them, and re-layouts: 23.6 us -> 0.01 us
    all_to_all x6 -> x0, other arithmetic: 17.2 us -> none  [the longest x1 4.93 us: shards(): lax.all_to_all(shell_imag, 'grp', split_axis=2, concat_axis=3, tiled=True)]
    all_to_all x14 -> x0, local copies, waits for them, and re-layouts: 8.73 us -> none  [the longest x2 2.44 us: shards(): lax.all_to_all(shell_imag, 'grp', split_axis=2, concat_axis=3, tiled=True)]
  transfers between devices with their start and end apart: 8 -> 0, of which waited for: 8 -> 0; matrix products, arithmetic and copies ran while one was open for 13% -> 0% of each run, Pallas kernels for 0% -> 0%
where the time goes in v1:
time: 100 us
  Pallas kernels  89.5 us (90%)
  between operations  7.27 us (7%)
  local copies, waits for them, and re-layouts  1.98 us (2%)
  other arithmetic  1.28 us (1%)
    pallas_call x1, Pallas kernels, shards(): pl.pallas_call(lambda *refs: kernel(slab_count, *refs), out_shape=jax.Sha...  89.5 us

profile of v1, /device:TPU:1, one launch (start us, length us, event | category | flops | bytes accessed | tf_op | source)
XLA Modules:
  0.0 100.0 jit_solution(9144984488749664647)
XLA Ops:
  0.0 0.7 convert_sqrt_fusion
  0.7 0.1 multiply_power_fusion
  0.7 0.6 fusion.2
  3.0 0.0 copy-start
  3.0 89.5 %shard_map.82 = f32[1,128]{1,0:T(1,128)} custom-call(s32[3]{0:T(128)} %refs_0_.1, f32[4,256,512]{2,1,0:T(8,128)} %refs_1_.1, bf16[2,512,256]{2,1,0:T(8,128)(2,1)} %constant.12.clone.refs_2_, bf16[2,2,256,512]{3,2,1,0:T(8,128)(2,1)} %constant.28.clone.refs_3_, bf16[2,2,512,256]{3,2,1,0:T(8,128)(2,1)} %constant.29.clone.refs_4_, ...), custom_call_target="tpu_custom_call" | custom-call | tf_op jit(solution)/shard_map/pallas_call | solution.py:227
  92.5 1.4 %fusion.1 = (f32[1,1]{1,0:T(1,128)}, f32[1,1]{1,0:T(1,128)}, f32[1,1]{1,0:T(1,128)}, f32[1,1]{1,0:T(1,128)}) fusion(f32[1,128]{1,0:T(1,128)} %shard_map.82), kind=kLoop, calls=%fused_computation.9 | loop fusion | bytes 32 | tf_op jit(solution)/shard_map/slice | solution.py:254
  99.5 0.0 copy-done
  99.5 0.5 compare_select_fusion.3
  (1 shorter events, 0.0 us)
Async XLA Ops:
  3.0 96.5 %copy-start = (s32[64,3]{0,1:T(4,128)S(1)}, s32[64,3]{0,1:T(4,128)}, u32[]{:S(2)}) copy-start(s32[64,3]{0,1:T(4,128)} %param.10) | copy-start | bytes 2308

commit v2 on v1

v2 whole, which is shorter than its diff:
```python
import math

import jax
import jax.numpy as jnp
import numpy as np
from jax import lax
from jax.experimental import pallas as pl
from jax.experimental.pallas import tpu as pltpu
from jax.sharding import PartitionSpec as P

MESH = pl.DeviceIdType.MESH
LANES = 128
SUB = 8
STEP = 37
CHUNKS = 4
USED = 6


def halves(table):
    table = np.asarray(table, np.float32)
    high = table.astype(jnp.bfloat16)
    low = (table - high.astype(np.float32)).astype(jnp.bfloat16)
    return np.stack([high, low])


def tables(length, kept, coarse):
    depth = kept // 2
    line = np.arange(length)
    wave = np.arange(kept)
    wave = np.where(wave < depth, wave, wave - kept)
    deep = np.arange(depth)
    points = np.arange(coarse)

    def angle(left, right, period):
        return 2.0 * np.pi / period * (left[:, None] * right[None, :] % period)

    a = angle(line, deep, length)
    depth_in = np.concatenate([np.cos(a), -np.sin(a)], 1)
    a = angle(wave, line, length)
    forward = np.stack([np.cos(a), np.sin(a)])
    a = angle(points, wave, coarse)
    inverse = np.stack([np.cos(a), np.sin(a)])
    a = angle(deep, points, coarse)
    weight = np.where(deep == 0, 1.0, 2.0)[:, None]
    depth_out = np.concatenate([weight * np.cos(a), -weight * np.sin(a)], 0)
    return [halves(t) for t in (depth_in, forward, inverse, depth_out)]


def split(x):
    high = x.astype(jnp.bfloat16)
    return high, (x - high.astype(jnp.float32)).astype(jnp.bfloat16)


def dot(left, right):
    def part(i, j):
        return jnp.dot(left[i], right[j], preferred_element_type=jnp.float32)

    return part(0, 0) + (part(0, 1) + part(1, 0))


def both(ref, index, columns=slice(None)):
    return ref[0, index, :, columns], ref[1, index, :, columns]


def where_is(y, z, x, core):
    return (lax.rem(y, 2) * 64 + (z * 4 + x) * 2 + core, lax.div(y, 2))


def kernel(
    edges, triangles, density, depth_in_hbm, forward_hbm, inverse_hbm, depth_out_hbm,
    out_ref,
    x_ref, depth_in, forward, inverse, depth_out,
    send1, recv1, send2, recv2, send3, recv3, lines, other_lines, send4, recv4, send5, recv5,
    load_sems, send_sems, chunk_sems, recv_sems, line_send_sems, line_recv_sems,
):
    slab, grp = lax.axis_index("slab"), lax.axis_index("grp")
    core = lax.rem(slab, 2)
    x = lax.rem(lax.div(slab, 2), 4)
    z = lax.rem(lax.div(slab, 8), 8)
    y = 2 * grp + lax.div(slab, 64)
    rest = lax.rem(slab, 64)
    chip = 64 * grp + lax.div(slab, 2)
    turn = core * 32 + lax.rem(z, 2) * 16 + lax.div(z, 2) * 4 + x
    slot = 64 * y + turn
    planes, half, length = x_ref.shape
    kept = forward.shape[2]
    devices, chips = kept, kept // 2

    copies = [(depth_in_hbm, depth_in), (density.at[0], x_ref.at[0]), (forward_hbm, forward)]
    copies += [(density.at[i], x_ref.at[i]) for i in range(1, planes)]
    copies += [(inverse_hbm, inverse), (depth_out_hbm, depth_out)]
    loads = [pltpu.make_async_copy(a, b, load_sems.at[n]) for n, (a, b) in enumerate(copies)]
    for load in loads:
        load.start()

    barrier = pltpu.get_barrier_semaphore()

    def greet(where):
        pl.semaphore_signal(barrier, inc=1, device_id=where, device_id_type=MESH)

    def of_rest(other):
        return where_is(y, lax.div(other, 8), lax.rem(lax.div(other, 2), 4), lax.rem(other, 2))

    def greet_rest(t, carry):
        greet(of_rest(lax.rem(rest + t, 64)))
        return carry

    with jax.named_scope("greet"):
        for step in range(1, 4):
            greet(where_is(lax.rem(y + step, 4), z, x, core))
        lax.fori_loop(1, 64, greet_rest, 0)

    with jax.named_scope("fwd"):
        loads[0].wait()
        loads[1].wait()
        loads[2].wait()
        table_in = (depth_in[0], depth_in[1])
        mine = pl.ds(pl.multiple_of(grp * half, half), half)
        cosine, sine = both(forward, 0, mine), both(forward, 1, mine)
        rows = send1.reshape(devices * SUB, LANES)
        for i in range(planes):
            if i:
                loads[2 + i].wait()
            modes = split(dot(split(x_ref[i]), table_in))
            c, s = dot(cosine, modes), dot(sine, modes)
            rows[pl.ds(2 * i, kept, stride=SUB), :] = c[:, :LANES] + s[:, LANES:]
            rows[pl.ds(2 * i + 1, kept, stride=SUB), :] = c[:, LANES:] - s[:, :LANES]

    with jax.named_scope("bar"):
        pl.semaphore_wait(barrier, 66)

    size = 64 // CHUNKS
    for j in range(CHUNKS):
        target = recv1.at[pl.ds(64 * y + size * j, size)]
        pltpu.make_async_copy(send1.at[pl.ds(64 * y + size * j, size)], target, chunk_sems.at[j]).start()
        for step in range(1, 4):
            other = lax.rem(y + step, 4)
            pltpu.make_async_remote_copy(
                src_ref=send1.at[pl.ds(64 * other + size * j, size)],
                dst_ref=target,
                send_sem=send_sems.at[0],
                recv_sem=chunk_sems.at[j],
                device_id=where_is(other, z, x, core),
                device_id_type=MESH,
            ).start()
    for j in range(CHUNKS):
        with jax.named_scope(f"ring_{j}"):
            everything = recv1.at[pl.ds(0, 4 * size)]
            pltpu.make_async_copy(everything, everything, chunk_sems.at[j]).wait()
        with jax.named_scope(f"push_{j}"):
            for low in range(2):
                first = recv1[64 * low + size * j : 64 * low + size * (j + 1)]
                second = recv1[64 * (low + 2) + size * j : 64 * (low + 2) + size * (j + 1)]
                send2[low, size * j : size * (j + 1)] = first + second

            def push(u, carry, j=j):
                t = size * j + lax.rem(u + 5 * rest, size)
                to_core = lax.div(t, 32)
                to_z = 2 * lax.div(lax.rem(t, 16), 4) + lax.rem(lax.div(t, 16), 2)
                to_x = lax.rem(t, 4)

                @pl.when(t != turn)
                def _():
                    pltpu.make_async_remote_copy(
                        src_ref=send2.at[:, t],
                        dst_ref=recv2.at[:, rest],
                        send_sem=send_sems.at[1],
                        recv_sem=recv_sems.at[0],
                        device_id=where_is(y, to_z, to_x, to_core),
                        device_id_type=MESH,
                    ).start()

                @pl.when(t == turn)
                def _():
                    pltpu.make_async_copy(send2.at[:, t], recv2.at[:, rest], recv_sems.at[0]).start()

                return carry

            lax.fori_loop(0, size, push, 0)
    with jax.named_scope("wait_two"):
        pltpu.make_async_copy(recv2, recv2, recv_sems.at[0]).wait()

    def joined(part):
        flat = recv2.reshape(2 * 64 * SUB, LANES)
        return flat[pl.ds(part, length, stride=2), :]

    radius = [jnp.sqrt(jnp.full((1, LANES), edges[n], jnp.int32).astype(jnp.float32)) for n in range(3)]
    volumes = [4.0 * math.pi / 3.0 * (radius[n + 1] ** 3 - radius[n] ** 3) for n in range(2)]
    with jax.named_scope("mid"):
        line = split(jnp.concatenate([joined(0), joined(1)], 1))
        c, s = dot(both(forward, 0), line), dot(both(forward, 1), line)
        real, imag = c[:, :LANES] + s[:, LANES:], c[:, LANES:] - s[:, :LANES]
        row = lax.broadcasted_iota(jnp.int32, real.shape, 0)
        first = jnp.where(row < kept // 2, row, row - kept)
        second = jnp.where(slot < kept // 2, slot, slot - kept)
        third = lax.broadcasted_iota(jnp.int32, real.shape, 1)
        squared = first * first + second * second + third * third
        loads[3 + planes - 1].wait()
        cosine, sine = both(inverse, 0), both(inverse, 1)
        flat = send3.reshape(devices * SUB, LANES)
    for n in range(2):
        with jax.named_scope(f"back_{n}"):
            scale = lax.rsqrt(float(length) ** 3 * volumes[n])
            inside = (squared >= edges[n]) & (squared < edges[n + 1])
            weight = jnp.where(inside, jnp.broadcast_to(scale, real.shape), 0.0)
            shell = split(jnp.concatenate([real * weight, imag * weight], 1))
            c, s = dot(cosine, shell), dot(sine, shell)
            back_real, back_imag = c[:, :LANES] - s[:, LANES:], c[:, LANES:] + s[:, :LANES]
            for p in range(3):
                these = slice(p * chips, (p + 1) * chips)
                flat[pl.ds(n * chips * SUB + 2 * p, chips, stride=SUB), :] = back_real[these]
                flat[pl.ds(n * chips * SUB + 2 * p + 1, chips, stride=SUB), :] = back_imag[these]
        with jax.named_scope(f"send_{n}"):

            def give(t, carry, n=n):
                to = lax.rem(chip + t * STEP, chips)
                pltpu.make_async_remote_copy(
                    src_ref=send3.at[n * chips + to, pl.ds(0, USED)],
                    dst_ref=recv3.at[slot, pl.ds(0, USED)],
                    send_sem=send_sems.at[2],
                    recv_sem=recv_sems.at[1],
                    device_id=(2 * lax.rem(to, 64) + n, lax.div(to, 64)),
                    device_id_type=MESH,
                ).start()
                return carry

            lax.fori_loop(1, chips, give, 0)

            @pl.when(core != n)
            def _(n=n, give=give):
                give(0, 0)

            @pl.when(core == n)
            def _(n=n):
                pltpu.make_async_copy(
                    send3.at[n * chips + chip, pl.ds(0, USED)], recv3.at[slot, pl.ds(0, USED)], recv_sems.at[1]
                ).start()

    with jax.named_scope("wait_three"):
        used = recv3.at[:, pl.ds(0, USED)]
        pltpu.make_async_copy(used, used, recv_sems.at[1]).wait()

    coarse = inverse.shape[2]
    part = coarse // 2
    with jax.named_scope("inv"):
        loads[3 + planes].wait()
        table_out = (depth_out[0], depth_out[1])
        flat = recv3.reshape(devices * SUB, LANES)
        swaps = []
        keep = pl.ds(pl.multiple_of(core * part, SUB), part)
        give_away = pl.ds(pl.multiple_of((1 - core) * part, SUB), part)
        for p in range(3):
            plane = split(
                jnp.concatenate(
                    [flat[pl.ds(2 * p, kept, stride=SUB), :], flat[pl.ds(2 * p + 1, kept, stride=SUB), :]], 1
                )
            )
            c, s = dot(cosine, plane), dot(sine, plane)
            lines[p] = jnp.concatenate([c[:, :LANES] - s[:, LANES:], c[:, LANES:] + s[:, :LANES]], 1)
            swap = pltpu.make_async_remote_copy(
                src_ref=lines.at[p, give_away],
                dst_ref=other_lines.at[p],
                send_sem=line_send_sems.at[p],
                recv_sem=line_recv_sems.at[p],
                device_id=where_is(y, z, x, 1 - core),
                device_id_type=MESH,
            )
            swap.start()
            swaps.append(swap)
        totals = [0.0] * 4
        owns = [dot(split(lines[p, keep]), table_out) for p in range(3)]
        for p in range(3):
            swaps[p].wait()
            own = owns[p]
            other = dot(split(other_lines[p]), table_out)
            own2, other2 = own * own, other * other
            for n, product in enumerate((own2 * own, own2 * other, other2 * own, other2 * other)):
                folded = jnp.sum(product.reshape(-1, SUB, coarse), 0)
                totals[n] = totals[n] + sum(folded[:, k : k + LANES] for k in range(0, coarse, LANES))
        lane = lax.broadcasted_iota(jnp.int32, (1, LANES), 1)
        packed = jnp.zeros((1, LANES), jnp.float32)
        for n in range(4):
            packed = jnp.where(lane == n + core * (3 - 2 * n), jnp.sum(totals[n], keepdims=True), packed)

    def gather(values, send, recv, n, place, where):
        send[0] = values
        recv[pl.ds(place, 1)] = values[None]

        def tell(t, carry):
            pltpu.make_async_remote_copy(
                src_ref=send,
                dst_ref=recv.at[pl.ds(place, 1)],
                send_sem=send_sems.at[n],
                recv_sem=recv_sems.at[n - 1],
                device_id=where(lax.rem(place + t, 16)),
                device_id_type=MESH,
            ).start()
            return carry

        lax.fori_loop(1, 16, tell, 0)
        others = recv.at[pl.ds(0, 15)]
        pltpu.make_async_copy(others, others, recv_sems.at[n - 1]).wait()
        return jnp.sum(recv[...], 0)

    with jax.named_scope("sum_one"):
        packed = gather(packed, send4, recv4, 3, 4 * y + x, lambda g: where_is(lax.div(g, 4), z, lax.rem(g, 4), core))
    with jax.named_scope("sum_two"):
        packed = gather(packed, send5, recv5, 4, 2 * z + core, lambda g: where_is(y, lax.div(g, 2), x, lax.rem(g, 2)))

    norms = []
    for volume in volumes:
        root = jnp.exp(jnp.log(volume) * (1.0 / 6.0))
        fifth = root * root * root * root * root
        norms.append(root - (fifth * root - volume) / (6.0 * fifth))
    finer = (float(length) / float(coarse)) ** 3 / float(length) ** 3
    ones = triangles[0:1] + triangles[1:2] + triangles[2:3]
    count = ones.shape[1]
    out = jnp.zeros(ones.shape, jnp.float32)
    for n in range(4):
        factor = finer
        for k in range(3):
            factor = factor * norms[1 if k < n else 0]
        value = jnp.broadcast_to(packed[:, n : n + 1], (1, count)) * factor[:, :count]
        out = jnp.where(ones == n, value, out)
    out_ref[...] = out

    for n, piece in (
        (0, send1.at[pl.ds(0, 192)]),
        (1, send1.at[pl.ds(0, 126)]),
        (2, send3.at[pl.ds(0, devices - 1), pl.ds(0, USED)]),
        (3, recv4.at[pl.ds(0, 15)]),
        (4, recv4.at[pl.ds(0, 15)]),
    ):
        pltpu.make_async_copy(piece, piece, send_sems.at[n]).wait()


def shards(density, shell_edges, triangles):
    planes, half, length = density.shape
    devices = 2 * lax.axis_size("slab")
    kept, coarse = length // 2, 3 * length // 4
    made = tables(length, kept, coarse)
    vmem = pl.BlockSpec(memory_space=pltpu.VMEM)
    hbm = pl.BlockSpec(memory_space=pl.ANY)
    tiles = pltpu.VMEM((devices, SUB, LANES), jnp.float32)
    pairs = pltpu.VMEM((2, 64, SUB, LANES), jnp.float32)
    row = pltpu.VMEM((1, 1, LANES), jnp.float32)
    sixteen = pltpu.VMEM((16, 1, LANES), jnp.float32)
    dma = pltpu.SemaphoreType.DMA
    out = pl.pallas_call(
        kernel,
        out_shape=jax.ShapeDtypeStruct((1, triangles.shape[0]), jnp.float32),
        in_specs=[pl.BlockSpec(memory_space=pltpu.SMEM), vmem] + [hbm] * 5,
        out_specs=vmem,
        scratch_shapes=[pltpu.VMEM(density.shape, jnp.float32)]
        + [pltpu.VMEM(t.shape, jnp.bfloat16) for t in made]
        + [tiles, tiles, pairs, pairs, tiles, tiles]
        + [
            pltpu.VMEM((3, coarse, 2 * LANES), jnp.float32),
            pltpu.VMEM((3, coarse // 2, 2 * LANES), jnp.float32),
        ]
        + [row, sixteen, row, sixteen]
        + [dma((planes + 4,)), dma((5,)), dma((CHUNKS,)), dma((4,)), dma((3,)), dma((3,))],
        compiler_params=pltpu.CompilerParams(
            collective_id=0, has_side_effects=True, vmem_limit_bytes=60 << 20
        ),
    )(shell_edges, triangles.T, density, *made)
    return out.reshape(-1)


def solution(mesh):
    return jax.shard_map(
        shards,
        mesh=mesh,
        in_specs=(P("slab", "grp", None), P(), P()),
        out_specs=P(),
        check_vma=False,
    )
```

time: 100 us -> 68.4 us (0.68)
  Pallas kernels: 89.5 us -> 67.1 us
  between operations: 7.27 us -> 0.01 us
  other arithmetic: 1.28 us -> 0 us
    pallas_call x1, Pallas kernels: 89.5 us -> 67.1 us  [shards(): pl.pallas_call(kernel, out_shape=jax.ShapeDtypeStruct((1, triangles.shape...]
    slice x2 -> x0, local copies, waits for them, and re-layouts: 1.98 us -> none  [the longest x1 1.38 us: shards(): sums[0, n] * norms[0] ** (3 - n) * norms[1] ** n * finer]
    unnamed x2 -> x1, local copies, waits for them, and re-layouts: 0.01 us -> 1.19 us
where the time goes in v2:
time: 68.4 us; the launch traced here: 68.3 us
  Pallas kernels  67.1 us (98%)
  local copies, waits for them, and re-layouts  1.19 us (2%)
    pallas_call x1, Pallas kernels, shards(): pl.pallas_call(kernel, out_shape=jax.ShapeDtypeStruct((1, triangles.shape...  67.1 us

profile of v2, /device:TPU:1, one launch (start us, length us, event | category | flops | bytes accessed | tf_op | source)
XLA Modules:
  0.0 68.3 jit_solution(14955106186971373540)
XLA Ops:
  0.0 67.1 %shard_map.73 = f32[1,64]{1,0:T(1,128)} custom-call(s32[3]{0:T(128)} %edges.1, s32[3,64]{1,0:T(4,128)} %bitcast.2, f32[4,256,512]{2,1,0:T(8,128)} %density.1, bf16[2,512,256]{2,1,0:T(8,128)(2,1)} %constant.8.clone.depth_in_hbm, bf16[2,2,256,512]{3,2,1,0:T(8,128)(2,1)} %constant.9.clone.forward_hbm, bf16[2,2,384,256]{3,2,1,0:T(8,128)(2,1)} %constant.10.clone.inverse_hbm, ...), custom_call_target="tpu_custom_call" | custom-call | tf_op jit(solution)/shard_map/pallas_call | solution.py:349
  67.1 1.2 %copy.9 = f32[64]{0:T(128)} copy(f32[64]{0:T(128)} %bitcast.3) | data formatting | bytes 512

commit v3 on v2

v3 whole, which is shorter than its diff:
```python
import math

import jax
import jax.numpy as jnp
import numpy as np
from jax import lax
from jax.experimental import pallas as pl
from jax.experimental.pallas import tpu as pltpu
from jax.sharding import PartitionSpec as P

MESH = pl.DeviceIdType.MESH
LANES = 128
SUB = 8
STEP = 13
CHUNKS = 8
FIRST, REST = 2, 4


def halves(table):
    table = np.asarray(table, np.float32)
    high = table.astype(jnp.bfloat16)
    low = (table - high.astype(np.float32)).astype(jnp.bfloat16)
    return np.stack([high, low])


def tables(length, kept, coarse):
    depth = kept // 2
    line = np.arange(length)
    wave = np.arange(kept)
    wave = np.where(wave < depth, wave, wave - kept)
    deep = np.arange(depth)
    points = np.arange(coarse)

    def angle(left, right, period):
        return 2.0 * np.pi / period * (left[:, None] * right[None, :] % period)

    a = angle(line, deep, length)
    depth_in = np.concatenate([np.cos(a), -np.sin(a)], 1)
    a = angle(wave, line, length)
    forward = np.stack([np.cos(a), np.sin(a)])
    a = angle(points, wave, coarse)
    inverse = np.stack([np.cos(a), np.sin(a)])
    a = angle(deep, points, coarse)
    weight = np.where(deep == 0, 1.0, 2.0)[:, None]
    depth_out = np.concatenate([weight * np.cos(a), -weight * np.sin(a)], 0)
    return [halves(t) for t in (depth_in, forward, inverse, depth_out)]


def split(x):
    high = x.astype(jnp.bfloat16)
    return high, (x - high.astype(jnp.float32)).astype(jnp.bfloat16)


def dot(left, right):
    def part(i, j):
        return jnp.dot(left[i], right[j], preferred_element_type=jnp.float32)

    return part(0, 0) + (part(0, 1) + part(1, 0))


def stacked(ref, rows):
    return tuple(jnp.concatenate([ref[part, 0, rows], ref[part, 1, rows]], 0) for part in range(2))


def where_is(y, z, x, core):
    return (lax.rem(y, 2) * 64 + (z * 4 + x) * 2 + core, lax.div(y, 2))


def kernel(
    edges, triangles, density, depth_in_hbm, forward_hbm, inverse_hbm, depth_out_hbm,
    out_ref,
    x_ref, modes, share, depth_in, forward, inverse, depth_out,
    send1, recv1, send2, recv2, send3, recv3, lines, other_lines, send4, recv4, send5, recv5,
    load_sems, send_sems, chunk_sems, recv_sems, line_sems,
):
    slab, grp = lax.axis_index("slab"), lax.axis_index("grp")
    core = lax.rem(slab, 2)
    x = lax.rem(lax.div(slab, 2), 4)
    z = lax.rem(lax.div(slab, 8), 8)
    y = 2 * grp + lax.div(slab, 64)
    rest = lax.rem(slab, 64)
    column = lax.div(slab, 2)
    chip = 64 * grp + column
    mine_j = 4 * core + lax.rem(x + 8 - z, 4)
    slot = 32 * mine_j + 8 * y + z
    planes, half, length = x_ref.shape
    kept = forward.shape[2]
    devices, chips = kept, kept // 2

    mine = pl.ds(pl.multiple_of(grp * half, half), half)
    pair = planes // 2
    copies = [
        (depth_in_hbm, depth_in),
        (density.at[pl.ds(0, pair)], x_ref.at[pl.ds(0, pair)]),
        (forward_hbm.at[:, :, :, mine], share),
        (density.at[pl.ds(pair, pair)], x_ref.at[pl.ds(pair, pair)]),
        (forward_hbm, forward),
        (inverse_hbm, inverse),
        (depth_out_hbm, depth_out),
    ]
    loads = [pltpu.make_async_copy(a, b, load_sems.at[n]) for n, (a, b) in enumerate(copies)]
    for load in loads[:4]:
        load.start()

    barrier = pltpu.get_barrier_semaphore()

    def greet(where):
        pl.semaphore_signal(barrier, inc=1, device_id=where, device_id_type=MESH)

    with jax.named_scope("greet"):
        for step_z in (4, 5, 3, 6, 2, 7, 1, 0):
            to_z = lax.rem(z + step_z, 8)

            def greet_plane(t, carry, to_z=to_z):
                greet(where_is(y, to_z, lax.rem(x + lax.div(t, 2), 4), lax.rem(core + t, 2)))
                return carry

            lax.fori_loop(0 if step_z else 1, 8, greet_plane, 0)
        for step in range(1, 4):
            greet(where_is(lax.rem(y + step, 4), z, x, core))

    with jax.named_scope("fwd"):
        loads[0].wait()
        loads[1].wait()
        loads[2].wait()
        table_in = (depth_in[0], depth_in[1])
        for i in range(planes):
            if i == pair:
                loads[3].wait()
            modes[i, 0], modes[i, 1] = split(dot(split(x_ref[i]), table_in))

    rows = send1.reshape(devices * SUB, LANES)
    size = 64 // CHUNKS
    wide = 4 * size
    for h in range(2):
        with jax.named_scope(f"fwd_{h}"):
            part = kept // 2
            table = stacked(share, slice(h * part, (h + 1) * part))
            for i in range(planes):
                out = dot(table, (modes[i, 0], modes[i, 1]))
                c, s = out[:part], out[part:]
                start = h * part * SUB + 2 * i
                rows[pl.ds(start, part, stride=SUB), :] = c[:, :LANES] + s[:, LANES:]
                rows[pl.ds(start + 1, part, stride=SUB), :] = c[:, LANES:] - s[:, :LANES]
        if h == 0:
            for load in loads[4:]:
                load.start()
            with jax.named_scope("bar"):
                pl.semaphore_wait(barrier, 66)
        for j in range(h * CHUNKS // 2, (h + 1) * CHUNKS // 2):
            target = recv1.at[pl.ds(64 * y + size * j, size)]
            for step in range(1, 4):
                other = lax.rem(y + step, 4)
                pltpu.make_async_remote_copy(
                    src_ref=send1.at[pl.ds(wide * j + size * other, size)],
                    dst_ref=target,
                    send_sem=send_sems.at[0],
                    recv_sem=chunk_sems.at[j],
                    device_id=where_is(other, z, x, core),
                    device_id_type=MESH,
                ).start()
            pltpu.make_async_copy(send1.at[pl.ds(wide * j + size * y, size)], target, chunk_sems.at[j]).start()

    for j in range(CHUNKS):
        with jax.named_scope(f"ring_{j}"):
            everything = recv1.at[pl.ds(0, 4 * size)]
            pltpu.make_async_copy(everything, everything, chunk_sems.at[j]).wait()
        with jax.named_scope(f"push_{j}"):
            for low in range(2):
                first = recv1[64 * low + size * j : 64 * low + size * (j + 1)]
                second = recv1[64 * (low + 2) + size * j : 64 * (low + 2) + size * (j + 1)]
                send2[low, size * j : size * (j + 1)] = first + second

            def push(u, carry, j=j):
                to_z = lax.rem(z + 3 * u, 8)
                pltpu.make_async_remote_copy(
                    src_ref=send2.at[:, size * j + to_z],
                    dst_ref=recv2.at[:, rest],
                    send_sem=send_sems.at[1],
                    recv_sem=recv_sems.at[0],
                    device_id=where_is(y, to_z, lax.rem(to_z + j, 4), j // 4),
                    device_id_type=MESH,
                ).start()
                return carry

            lax.fori_loop(1, size, push, 0)

            @pl.when(mine_j != j)
            def _(push=push):
                push(0, 0)

            @pl.when(mine_j == j)
            def _(j=j):
                pltpu.make_async_copy(send2.at[:, size * j + z], recv2.at[:, rest], recv_sems.at[0]).start()

    with jax.named_scope("wait_two"):
        pltpu.make_async_copy(recv2, recv2, recv_sems.at[0]).wait()

    def joined(part):
        flat = recv2.reshape(2 * 64 * SUB, LANES)
        return flat[pl.ds(part, length, stride=2), :]

    radius = [jnp.sqrt(jnp.full((1, LANES), edges[n], jnp.int32).astype(jnp.float32)) for n in range(3)]
    volumes = [4.0 * math.pi / 3.0 * (radius[n + 1] ** 3 - radius[n] ** 3) for n in range(2)]
    with jax.named_scope("mid"):
        loads[4].wait()
        line = split(jnp.concatenate([joined(0), joined(1)], 1))
        out = dot(stacked(forward, slice(None)), line)
        c, s = out[:kept], out[kept:]
        real, imag = c[:, :LANES] + s[:, LANES:], c[:, LANES:] - s[:, :LANES]
        row = lax.broadcasted_iota(jnp.int32, real.shape, 0)
        first = jnp.where(row < kept // 2, row, row - kept)
        second = jnp.where(slot < kept // 2, slot, slot - kept)
        third = lax.broadcasted_iota(jnp.int32, real.shape, 1)
        squared = first * first + second * second + third * third
        weighted = []
        for n in range(2):
            scale = lax.rsqrt(float(length) ** 3 * volumes[n])
            inside = (squared >= edges[n]) & (squared < edges[n + 1])
            weight = jnp.where(inside, jnp.broadcast_to(scale, real.shape), 0.0)
            weighted += [real * weight, imag * weight]
        shells = split(jnp.concatenate(weighted, 1))
        loads[5].wait()

    def planes_back(start, count):
        out = dot(stacked(inverse, slice(start, start + count)), shells)
        c, s = out[:count], out[count:]
        for n in range(2):
            re, im = 2 * n * LANES, (2 * n + 1) * LANES
            yield c[:, re : re + LANES] - s[:, im : im + LANES]
            yield c[:, im : im + LANES] + s[:, re : re + LANES]

    flat = send3.reshape(devices * SUB, LANES)

    def give_all(start, count, recv_n):
        these = pl.ds(start, count)

        def give(n, place, to_grp):
            pltpu.make_async_remote_copy(
                src_ref=send3.at[n * chips + to_grp * 64 + place, these],
                dst_ref=recv3.at[slot, these],
                send_sem=send_sems.at[2],
                recv_sem=recv_sems.at[recv_n],
                device_id=(2 * place + n, to_grp),
                device_id_type=MESH,
            ).start()

        def give_four(t, carry):
            place = lax.rem(column + t * STEP, 64)
            for n in range(2):
                give(n, place, grp)
                give(n, place, 1 - grp)
            return carry

        lax.fori_loop(1, 64, give_four, 0)
        for n in range(2):
            give(n, column, 1 - grp)

            @pl.when(core != n)
            def _(n=n):
                give(n, column, grp)

            @pl.when(core == n)
            def _(n=n):
                pltpu.make_async_copy(
                    send3.at[n * chips + chip, these], recv3.at[slot, these], recv_sems.at[recv_n]
                ).start()

    with jax.named_scope("back_0"):
        for k, piece in enumerate(planes_back(2 * chips, chips)):
            n, imaginary = k // 2, k % 2
            flat[pl.ds(n * chips * SUB + imaginary, chips, stride=SUB), :] = piece
    with jax.named_scope("send_0"):
        give_all(0, FIRST, 1)
    with jax.named_scope("back_1"):
        for k, piece in enumerate(planes_back(0, 2 * chips)):
            for n in range(2):
                start = n * chips * SUB + FIRST + k
                flat[pl.ds(start, chips, stride=SUB), :] = piece[n * chips : (n + 1) * chips]
    with jax.named_scope("send_1"):
        give_all(FIRST, REST, 4)

    coarse = inverse.shape[2]
    part = coarse // 2
    flat = recv3.reshape(devices * SUB, LANES)
    rows_out = stacked(inverse, slice(None))

    def to_lines(row):
        plane = jnp.concatenate(
            [flat[pl.ds(row, kept, stride=SUB), :], flat[pl.ds(row + 1, kept, stride=SUB), :]], 1
        )
        out = dot(rows_out, split(plane))
        c, s = out[:coarse], out[coarse:]
        return jnp.concatenate([c[:, :LANES] - s[:, LANES:], c[:, LANES:] + s[:, :LANES]], 1)

    def to_field(values):
        return dot(split(values), (depth_out[0], depth_out[1]))

    def triple_sums(f, g):
        ff, gg = f * f, g * g
        for product in (ff * f, ff * g, gg * f, gg * g):
            folded = jnp.sum(product.reshape(-1, SUB, coarse), 0)
            yield sum(folded[:, k : k + LANES] for k in range(0, coarse, LANES))

    with jax.named_scope("wait_three"):
        arrived = recv3.at[:, pl.ds(0, FIRST)]
        pltpu.make_async_copy(arrived, arrived, recv_sems.at[1]).wait()
        loads[6].wait()
    with jax.named_scope("inv_0"):
        lines[...] = to_lines(0)
        keep = pl.ds(pl.multiple_of(core * part, SUB), part)
        give_away = pl.ds(pl.multiple_of((1 - core) * part, SUB), part)
        swap = pltpu.make_async_remote_copy(
            src_ref=lines.at[give_away],
            dst_ref=other_lines,
            send_sem=line_sems.at[0],
            recv_sem=line_sems.at[1],
            device_id=where_is(y, z, x, 1 - core),
            device_id_type=MESH,
        )
        swap.start()
        own = to_field(lines[keep])
        swap.wait()
        shared = list(triple_sums(own, to_field(other_lines[...])))
    with jax.named_scope("wait_four"):
        arrived = recv3.at[:, pl.ds(FIRST, REST)]
        pltpu.make_async_copy(arrived, arrived, recv_sems.at[4]).wait()
    with jax.named_scope("inv_1"):
        whole = list(triple_sums(to_field(to_lines(FIRST)), to_field(to_lines(FIRST + 2))))
        lane = lax.broadcasted_iota(jnp.int32, (1, LANES), 1)
        packed = jnp.zeros((1, LANES), jnp.float32)
        for n in range(4):
            total = whole[n] + jnp.where(core == 0, shared[n], shared[3 - n])
            packed = jnp.where(lane == n, jnp.sum(total, keepdims=True), packed)

    def gather(values, send, recv, n, place, where):
        send[0] = values
        recv[pl.ds(place, 1)] = values[None]

        def tell(t, carry):
            pltpu.make_async_remote_copy(
                src_ref=send,
                dst_ref=recv.at[pl.ds(place, 1)],
                send_sem=send_sems.at[n],
                recv_sem=recv_sems.at[n - 1],
                device_id=where(lax.rem(place + t, 16)),
                device_id_type=MESH,
            ).start()
            return carry

        lax.fori_loop(1, 16, tell, 0)
        others = recv.at[pl.ds(0, 15)]
        pltpu.make_async_copy(others, others, recv_sems.at[n - 1]).wait()
        return jnp.sum(recv[...], 0)

    norms = []
    for volume in volumes:
        root = jnp.exp(jnp.log(volume) * (1.0 / 6.0))
        fifth = root * root * root * root * root
        norms.append(root - (fifth * root - volume) / (6.0 * fifth))
    factors = []
    for n in range(4):
        a, b, c = (norms[1 if k < n else 0] for k in range(3))
        factors.append(a * b * c)
    with jax.named_scope("sum_one"):
        packed = gather(packed, send4, recv4, 3, 4 * y + x, lambda g: where_is(lax.div(g, 4), z, lax.rem(g, 4), core))
    with jax.named_scope("sum_two"):
        packed = gather(packed, send5, recv5, 4, 2 * z + core, lambda g: where_is(y, lax.div(g, 2), x, lax.rem(g, 2)))

    ones = triangles[0:1] + triangles[1:2] + triangles[2:3]
    count = ones.shape[1]
    out = jnp.zeros(ones.shape, jnp.float32)
    for n in range(4):
        value = jnp.broadcast_to(packed[:, n : n + 1], (1, count)) * factors[n][:, :count]
        out = jnp.where(ones == n, value, out)
    out_ref[...] = out

    for n, piece in (
        (0, send1.at[pl.ds(0, 192)]),
        (1, send1.at[pl.ds(0, 126)]),
        (2, send3.at[pl.ds(0, devices - 1), pl.ds(0, FIRST + REST)]),
        (3, recv4.at[pl.ds(0, 15)]),
        (4, recv4.at[pl.ds(0, 15)]),
    ):
        pltpu.make_async_copy(piece, piece, send_sems.at[n]).wait()


def shards(density, shell_edges, triangles):
    planes, half, length = density.shape
    devices = 2 * lax.axis_size("slab")
    kept, coarse = length // 2, 3 * length // 4
    made = tables(length, kept, coarse)
    vmem = pl.BlockSpec(memory_space=pltpu.VMEM)
    hbm = pl.BlockSpec(memory_space=pl.ANY)
    tiles = pltpu.VMEM((devices, SUB, LANES), jnp.float32)
    pairs = pltpu.VMEM((2, 64, SUB, LANES), jnp.float32)
    row = pltpu.VMEM((1, 1, LANES), jnp.float32)
    sixteen = pltpu.VMEM((16, 1, LANES), jnp.float32)
    dma = pltpu.SemaphoreType.DMA
    out = pl.pallas_call(
        kernel,
        out_shape=jax.ShapeDtypeStruct((1, triangles.shape[0]), jnp.float32),
        in_specs=[pl.BlockSpec(memory_space=pltpu.SMEM), vmem] + [hbm] * 5,
        out_specs=vmem,
        scratch_shapes=[
            pltpu.VMEM(density.shape, jnp.float32),
            pltpu.VMEM((planes, 2, half, 2 * LANES), jnp.bfloat16),
            pltpu.VMEM((2, 2, kept, half), jnp.bfloat16),
        ]
        + [pltpu.VMEM(t.shape, jnp.bfloat16) for t in made]
        + [tiles, tiles, pairs, pairs, tiles, tiles]
        + [
            pltpu.VMEM((coarse, 2 * LANES), jnp.float32),
            pltpu.VMEM((coarse // 2, 2 * LANES), jnp.float32),
        ]
        + [row, sixteen, row, sixteen]
        + [dma((7,)), dma((5,)), dma((CHUNKS,)), dma((5,)), dma((2,))],
        compiler_params=pltpu.CompilerParams(
            collective_id=0, has_side_effects=True, vmem_limit_bytes=60 << 20
        ),
    )(shell_edges, triangles.T, density, *made)
    return out.reshape(-1) * (1.0 / float(coarse) ** 3)


def solution(mesh):
    return jax.shard_map(
        shards,
        mesh=mesh,
        in_specs=(P("slab", "grp", None), P(), P()),
        out_specs=P(),
        check_vma=False,
    )
```

time: 68.4 us -> 65 us (0.950)
  Pallas kernels: 67.1 us -> 63.7 us
  other arithmetic: 0 us -> 1.19 us
  local copies, waits for them, and re-layouts: 1.19 us -> 0 us
    pallas_call x1, Pallas kernels: 67.1 us -> 63.7 us  [shards(): pl.pallas_call(kernel, out_shape=jax.ShapeDtypeStruct((1, triangles.shape...]
    mul x0 -> x1, other arithmetic: none -> 1.19 us  [shards(): return out.reshape(-1) * (1.0 / float(coarse) ** 3)]
    unnamed x1 -> x0, local copies, waits for them, and re-layouts: 1.19 us -> none
where the time goes in v3:
time: 65 us; the launch traced here: 64.9 us
  Pallas kernels  63.7 us (98%)
  other arithmetic  1.19 us (2%)
    pallas_call x1, Pallas kernels, shards(): pl.pallas_call(kernel, out_shape=jax.ShapeDtypeStruct((1, triangles.shape...  63.7 us

profile of v3, /device:TPU:1, one launch (start us, length us, event | category | flops | bytes accessed | tf_op | source)
XLA Modules:
  0.0 64.9 jit_solution(15420217312142914540)
XLA Ops:
  0.0 63.7 %shard_map.73 = f32[1,64]{1,0:T(1,128)} custom-call(s32[3]{0:T(128)} %edges.1, s32[3,64]{1,0:T(4,128)} %bitcast.3, f32[4,256,512]{2,1,0:T(8,128)} %density.1, bf16[2,512,256]{2,1,0:T(8,128)(2,1)} %constant.10.clone.depth_in_hbm, bf16[2,2,256,512]{3,2,1,0:T(8,128)(2,1)} %constant.11.clone.forward_hbm, bf16[2,2,384,256]{3,2,1,0:T(8,128)(2,1)} %constant.12.clone.inverse_hbm, ...), custom_call_target="tpu_custom_call" | custom-call | tf_op jit(solution)/shard_map/pallas_call | solution.py:400
  63.7 1.2 %multiply_bitcast_fusion = f32[64]{0:T(128)} fusion(f32[1,64]{1,0:T(1,128)} %shard_map.73), kind=kLoop, calls=%fused_computation | loop fusion | flops 64 | bytes 512 | tf_op jit(solution)/shard_map/mul | solution.py:422

commit v4 on v3

--- a/solution.py
+++ b/solution.py
@@ -11,7 +11,7 @@
 MESH = pl.DeviceIdType.MESH
 LANES = 128
 SUB = 8
-STEP = 13
+FAR_FIRST = (4, 5, 3, 6, 2, 7, 1, 0)
 CHUNKS = 8
 FIRST, REST = 2, 4
 
@@ -26,8 +26,7 @@
 def tables(length, kept, coarse):
     depth = kept // 2
     line = np.arange(length)
-    wave = np.arange(kept)
-    wave = np.where(wave < depth, wave, wave - kept)
+    wave = signed(np.arange(kept), kept, np.where)
     deep = np.arange(depth)
     points = np.arange(coarse)
 
@@ -36,14 +35,41 @@
 
     a = angle(line, deep, length)
     depth_in = np.concatenate([np.cos(a), -np.sin(a)], 1)
-    a = angle(wave, line, length)
-    forward = np.stack([np.cos(a), np.sin(a)])
-    a = angle(points, wave, coarse)
-    inverse = np.stack([np.cos(a), np.sin(a)])
+    a = angle(wave, line[:kept], length)
+    second_in = np.stack([np.cos(a), np.sin(a)])
+    evens_first = by_parity(np.arange(kept), kept, np.where)
+    a = angle(evens_first, line[:kept], length).reshape(2, depth, kept)
+    first_in = np.concatenate([np.cos(a), np.sin(a)], 1)
+    a = angle(points, evens_first, coarse)
+    first_out = np.stack([np.cos(a), np.sin(a)])
+    a = np.stack([angle(points[: coarse // 2], wave[odd::2], coarse) for odd in range(2)])
+    second_out = np.stack([np.cos(a), np.sin(a)])
     a = angle(deep, points, coarse)
     weight = np.where(deep == 0, 1.0, 2.0)[:, None]
     depth_out = np.concatenate([weight * np.cos(a), -weight * np.sin(a)], 0)
-    return [halves(t) for t in (depth_in, forward, inverse, depth_out)]
+    return [halves(t) for t in (depth_in, second_in, first_in, first_out, second_out, depth_out)]
+
+
+def signed(index, kept, where):
+    wave = index + kept * 9 // 16
+    wave = where(wave < kept, wave, wave - kept)
+    return where(wave < kept // 2, wave, wave - kept)
+
+
+def by_parity(index, kept, where):
+    half = kept // 2
+    wave = where(index < half, 2 * index, 2 * (index - half) + 1)
+    return where(wave < half, wave, wave - kept)
+
+
+def folded(real, imag):
+    lane = lax.broadcasted_iota(jnp.int32, real.shape, 1)
+    return jnp.where(lane < LANES // 2, real, pltpu.roll(imag, LANES // 2, 1))
+
+
+def unfolded(row):
+    lane = lax.broadcasted_iota(jnp.int32, row.shape, 1)
+    return tuple(jnp.where(lane < LANES // 2, part, 0.0) for part in (row, pltpu.roll(row, LANES // 2, 1)))
 
 
 def split(x):
@@ -67,10 +93,10 @@
 
 
 def kernel(
-    edges, triangles, density, depth_in_hbm, forward_hbm, inverse_hbm, depth_out_hbm,
+    edges, triangles, density, depth_in_hbm, second_in_hbm, first_in_hbm, first_out_hbm, second_out_hbm, depth_out_hbm,
     out_ref,
-    x_ref, modes, share, depth_in, forward, inverse, depth_out,
-    send1, recv1, send2, recv2, send3, recv3, lines, other_lines, send4, recv4, send5, recv5,
+    x_ref, modes, depth_in, second_in, first_in, first_out, second_out, depth_out,
+    send1, recv1, send2, recv2, line_real, line_imag, send3, recv3, lines, other_lines, send4, recv4, send5, recv5,
     load_sems, send_sems, chunk_sems, recv_sems, line_sems,
 ):
     slab, grp = lax.axis_index("slab"), lax.axis_index("grp")
@@ -80,22 +106,25 @@
     y = 2 * grp + lax.div(slab, 64)
     rest = lax.rem(slab, 64)
     column = lax.div(slab, 2)
+    y_low = lax.div(slab, 64)
     chip = 64 * grp + column
     mine_j = 4 * core + lax.rem(x + 8 - z, 4)
     slot = 32 * mine_j + 8 * y + z
+    edge = mine_j == CHUNKS - 1
+    landing = lax.rem(slot, 2) * 128 + lax.div(slot, 2)
     planes, half, length = x_ref.shape
-    kept = forward.shape[2]
+    kept = second_in.shape[2]
     devices, chips = kept, kept // 2
 
-    mine = pl.ds(pl.multiple_of(grp * half, half), half)
     pair = planes // 2
     copies = [
         (depth_in_hbm, depth_in),
         (density.at[pl.ds(0, pair)], x_ref.at[pl.ds(0, pair)]),
-        (forward_hbm.at[:, :, :, mine], share),
+        (second_in_hbm, second_in),
         (density.at[pl.ds(pair, pair)], x_ref.at[pl.ds(pair, pair)]),
-        (forward_hbm, forward),
-        (inverse_hbm, inverse),
+        (first_in_hbm, first_in),
+        (first_out_hbm, first_out),
+        (second_out_hbm, second_out),
         (depth_out_hbm, depth_out),
     ]
     loads = [pltpu.make_async_copy(a, b, load_sems.at[n]) for n, (a, b) in enumerate(copies)]
@@ -108,7 +137,7 @@
         pl.semaphore_signal(barrier, inc=1, device_id=where, device_id_type=MESH)
 
     with jax.named_scope("greet"):
-        for step_z in (4, 5, 3, 6, 2, 7, 1, 0):
+        for step_z in FAR_FIRST:
             to_z = lax.rem(z + step_z, 8)
 
             def greet_plane(t, carry, to_z=to_z):
@@ -135,82 +164,111 @@
     for h in range(2):
         with jax.named_scope(f"fwd_{h}"):
             part = kept // 2
-            table = stacked(share, slice(h * part, (h + 1) * part))
+            table = stacked(second_in, slice(h * part, (h + 1) * part))
             for i in range(planes):
                 out = dot(table, (modes[i, 0], modes[i, 1]))
                 c, s = out[:part], out[part:]
+                real, imag = c[:, :LANES] + s[:, LANES:], c[:, LANES:] - s[:, :LANES]
                 start = h * part * SUB + 2 * i
-                rows[pl.ds(start, part, stride=SUB), :] = c[:, :LANES] + s[:, LANES:]
-                rows[pl.ds(start + 1, part, stride=SUB), :] = c[:, LANES:] - s[:, :LANES]
+                full = part - h * wide
+                rows[pl.ds(start, full, stride=SUB), :] = real[:full]
+                rows[pl.ds(start + 1, full, stride=SUB), :] = imag[:full]
+                if h:
+                    rows[pl.ds((kept - wide) * SUB + i, wide, stride=SUB), :] = folded(real[full:], imag[full:])
         if h == 0:
             for load in loads[4:]:
                 load.start()
             with jax.named_scope("bar"):
                 pl.semaphore_wait(barrier, 66)
         for j in range(h * CHUNKS // 2, (h + 1) * CHUNKS // 2):
-            target = recv1.at[pl.ds(64 * y + size * j, size)]
+            used = pl.ds(0, SUB if j < CHUNKS - 1 else SUB // 2)
+            target = recv1.at[pl.ds(64 * y + size * j, size), used]
             for step in range(1, 4):
                 other = lax.rem(y + step, 4)
                 pltpu.make_async_remote_copy(
-                    src_ref=send1.at[pl.ds(wide * j + size * other, size)],
+                    src_ref=send1.at[pl.ds(wide * j + size * other, size), used],
                     dst_ref=target,
                     send_sem=send_sems.at[0],
                     recv_sem=chunk_sems.at[j],
                     device_id=where_is(other, z, x, core),
                     device_id_type=MESH,
                 ).start()
-            pltpu.make_async_copy(send1.at[pl.ds(wide * j + size * y, size)], target, chunk_sems.at[j]).start()
+            pltpu.make_async_copy(
+                send1.at[pl.ds(wide * j + size * y, size), used], target, chunk_sems.at[j]
+            ).start()
 
     for j in range(CHUNKS):
+        height = SUB if j < CHUNKS - 1 else SUB // 2
+        used = pl.ds(0, height)
         with jax.named_scope(f"ring_{j}"):
-            everything = recv1.at[pl.ds(0, 4 * size)]
+            everything = recv1.at[pl.ds(0, 4 * size), used]
             pltpu.make_async_copy(everything, everything, chunk_sems.at[j]).wait()
+        index = lax.broadcasted_iota(jnp.int32, (size, height, LANES), 0)
+        sign = jnp.where(lax.rem(index, 2) == 0, 1.0, -1.0)
         with jax.named_scope(f"push_{j}"):
             for low in range(2):
-                first = recv1[64 * low + size * j : 64 * low + size * (j + 1)]
-                second = recv1[64 * (low + 2) + size * j : 64 * (low + 2) + size * (j + 1)]
-                send2[low, size * j : size * (j + 1)] = first + second
-
-            def push(u, carry, j=j):
-                to_z = lax.rem(z + 3 * u, 8)
+                first = recv1[64 * low + size * j : 64 * low + size * (j + 1), :height]
+                second = recv1[64 * (low + 2) + size * j : 64 * (low + 2) + size * (j + 1), :height]
+                send2[low, size * j : size * (j + 1), :height] = first + sign * second
+
+            def push(step_z, j=j, used=used):
+                to_z = lax.rem(z + step_z, 8)
                 pltpu.make_async_remote_copy(
-                    src_ref=send2.at[:, size * j + to_z],
-                    dst_ref=recv2.at[:, rest],
+                    src_ref=send2.at[:, size * j + to_z, used],
+                    dst_ref=recv2.at[:, rest, used],
                     send_sem=send_sems.at[1],
                     recv_sem=recv_sems.at[0],
                     device_id=where_is(y, to_z, lax.rem(to_z + j, 4), j // 4),
                     device_id_type=MESH,
                 ).start()
-                return carry
-
-            lax.fori_loop(1, size, push, 0)
+
+            for step_z in FAR_FIRST[:-1]:
+                push(step_z)
 
             @pl.when(mine_j != j)
             def _(push=push):
-                push(0, 0)
+                push(0)
 
             @pl.when(mine_j == j)
-            def _(j=j):
-                pltpu.make_async_copy(send2.at[:, size * j + z], recv2.at[:, rest], recv_sems.at[0]).start()
-
-    with jax.named_scope("wait_two"):
+            def _(j=j, used=used):
+                pltpu.make_async_copy(
+                    send2.at[:, size * j + z, used], recv2.at[:, rest, used], recv_sems.at[0]
+                ).start()
+
+    flat = recv2.reshape(2 * 64 * SUB, LANES)
+
+    @pl.when(jnp.logical_not(edge))
+    def _():
         pltpu.make_async_copy(recv2, recv2, recv_sems.at[0]).wait()
-
-    def joined(part):
-        flat = recv2.reshape(2 * 64 * SUB, LANES)
-        return flat[pl.ds(part, length, stride=2), :]
+        line_real[...] = flat[pl.ds(0, length, stride=2), :]
+        line_imag[...] = flat[pl.ds(1, length, stride=2), :]
+
+    @pl.when(edge)
+    def _():
+        used = recv2.at[:, :, pl.ds(0, SUB // 2)]
+        pltpu.make_async_copy(used, used, recv_sems.at[0]).wait()
+        for low in range(2):
+            for i in range(planes):
+                real, imag = unfolded(flat[pl.ds(low * 64 * SUB + i, 64, stride=SUB), :])
+                line_real[pl.ds(low * 64 * planes + i, 64, stride=planes), :] = real
+                line_imag[pl.ds(low * 64 * planes + i, 64, stride=planes), :] = imag
 
     radius = [jnp.sqrt(jnp.full((1, LANES), edges[n], jnp.int32).astype(jnp.float32)) for n in range(3)]
     volumes = [4.0 * math.pi / 3.0 * (radius[n + 1] ** 3 - radius[n] ** 3) for n in range(2)]
     with jax.named_scope("mid"):
         loads[4].wait()
-        line = split(jnp.concatenate([joined(0), joined(1)], 1))
-        out = dot(stacked(forward, slice(None)), line)
-        c, s = out[:kept], out[kept:]
-        real, imag = c[:, :LANES] + s[:, LANES:], c[:, LANES:] - s[:, :LANES]
+        line = jnp.concatenate([line_real[...], line_imag[...]], 1)
+        real, imag = [], []
+        for odd in range(2):
+            mixed = line[:kept] - line[kept:] if odd else line[:kept] + line[kept:]
+            out = dot((first_in[0, odd], first_in[1, odd]), split(mixed))
+            c, s = out[: kept // 2], out[kept // 2 :]
+            real.append(c[:, :LANES] + s[:, LANES:])
+            imag.append(c[:, LANES:] - s[:, :LANES])
+        real, imag = jnp.concatenate(real, 0), jnp.concatenate(imag, 0)
         row = lax.broadcasted_iota(jnp.int32, real.shape, 0)
-        first = jnp.where(row < kept // 2, row, row - kept)
-        second = jnp.where(slot < kept // 2, slot, slot - kept)
+        first = by_parity(row, kept, jnp.where)
+        second = signed(slot, kept, jnp.where)
         third = lax.broadcasted_iota(jnp.int32, real.shape, 1)
         squared = first * first + second * second + third * third
         weighted = []
@@ -223,7 +281,7 @@
         loads[5].wait()
 
     def planes_back(start, count):
-        out = dot(stacked(inverse, slice(start, start + count)), shells)
+        out = dot(stacked(first_out, slice(start, start + count)), shells)
         c, s = out[:count], out[count:]
         for n in range(2):
             re, im = 2 * n * LANES, (2 * n + 1) * LANES
@@ -238,21 +296,24 @@
         def give(n, place, to_grp):
             pltpu.make_async_remote_copy(
                 src_ref=send3.at[n * chips + to_grp * 64 + place, these],
-                dst_ref=recv3.at[slot, these],
+                dst_ref=recv3.at[landing, these],
                 send_sem=send_sems.at[2],
                 recv_sem=recv_sems.at[recv_n],
                 device_id=(2 * place + n, to_grp),
                 device_id_type=MESH,
             ).start()
 
-        def give_four(t, carry):
-            place = lax.rem(column + t * STEP, 64)
-            for n in range(2):
-                give(n, place, grp)
-                give(n, place, 1 - grp)
-            return carry
-
-        lax.fori_loop(1, 64, give_four, 0)
+        for step_z in FAR_FIRST:
+            to_z = lax.rem(z + step_z, 8)
+
+            def give_four(t, carry, to_z=to_z):
+                place = lax.rem(y_low + lax.div(t, 4), 2) * 32 + to_z * 4 + lax.rem(x + t, 4)
+                for n in range(2):
+                    give(n, place, 1 - grp)
+                    give(n, place, grp)
+                return carry
+
+            lax.fori_loop(0 if step_z else 1, 8, give_four, 0)
         for n in range(2):
             give(n, column, 1 - grp)
 
@@ -263,35 +324,68 @@
             @pl.when(core == n)
             def _(n=n):
                 pltpu.make_async_copy(
-                    send3.at[n * chips + chip, these], recv3.at[slot, these], recv_sems.at[recv_n]
+                    send3.at[n * chips + chip, these], recv3.at[landing, these], recv_sems.at[recv_n]
                 ).start()
 
     with jax.named_scope("back_0"):
-        for k, piece in enumerate(planes_back(2 * chips, chips)):
-            n, imaginary = k // 2, k % 2
-            flat[pl.ds(n * chips * SUB + imaginary, chips, stride=SUB), :] = piece
+        a, b, c, d = planes_back(2 * chips, chips)
+        for n, (real, imag) in enumerate(((a, b), (c, d))):
+            start = n * chips * SUB
+            flat[pl.ds(start, chips, stride=SUB), :] = jnp.where(edge, folded(real, imag), real)
+            flat[pl.ds(start + 1, chips, stride=SUB), :] = imag
     with jax.named_scope("send_0"):
-        give_all(0, FIRST, 1)
+
+        @pl.when(jnp.logical_not(edge))
+        def _():
+            give_all(0, FIRST, 1)
+
+        @pl.when(edge)
+        def _():
+            give_all(0, FIRST // 2, 1)
+
     with jax.named_scope("back_1"):
-        for k, piece in enumerate(planes_back(0, 2 * chips)):
+        a, b, c, d = planes_back(0, 2 * chips)
+        pieces = (jnp.where(edge, folded(a, b), a), jnp.where(edge, folded(c, d), b), c, d)
+        for k, piece in enumerate(pieces):
             for n in range(2):
                 start = n * chips * SUB + FIRST + k
                 flat[pl.ds(start, chips, stride=SUB), :] = piece[n * chips : (n + 1) * chips]
     with jax.named_scope("send_1"):
-        give_all(FIRST, REST, 4)
-
-    coarse = inverse.shape[2]
+
+        @pl.when(jnp.logical_not(edge))
+        def _():
+            give_all(FIRST, REST, 4)
+
+        @pl.when(edge)
+        def _():
+            give_all(FIRST, REST // 2, 4)
+
+    coarse = first_out.shape[2]
     part = coarse // 2
     flat = recv3.reshape(devices * SUB, LANES)
-    rows_out = stacked(inverse, slice(None))
-
-    def to_lines(row):
-        plane = jnp.concatenate(
-            [flat[pl.ds(row, kept, stride=SUB), :], flat[pl.ds(row + 1, kept, stride=SUB), :]], 1
-        )
-        out = dot(rows_out, split(plane))
-        c, s = out[:coarse], out[coarse:]
-        return jnp.concatenate([c[:, :LANES] - s[:, LANES:], c[:, LANES:] + s[:, :LANES]], 1)
+
+    full = (kept - wide) // 2
+
+    def to_lines(places):
+        sums = []
+        for odd in range(2):
+            start = odd * chips * SUB
+            columns = []
+            for row, edge_row in places:
+                whole = [flat[pl.ds(start + row + k, full, stride=SUB), :] for k in range(2)]
+                ends = unfolded(flat[pl.ds(start + full * SUB + edge_row, wide // 2, stride=SUB), :])
+                columns.append(jnp.concatenate([whole[0], ends[0], whole[1], ends[1]], 0))
+            sums.append(dot(line_tables[odd], split(jnp.concatenate(columns, 1))))
+        upper, lower = sums[0] + sums[1], sums[0] - sums[1]
+        for n in range(len(places)):
+            these = slice(n * LANES, (n + 1) * LANES)
+            yield jnp.concatenate(
+                [
+                    jnp.concatenate([upper[:part, these], upper[part:, these]], 1),
+                    jnp.concatenate([lower[:part, these], lower[part:, these]], 1),
+                ],
+                0,
+            )
 
     def to_field(values):
         return dot(split(values), (depth_out[0], depth_out[1]))
@@ -303,11 +397,21 @@
             yield sum(folded[:, k : k + LANES] for k in range(0, coarse, LANES))
 
     with jax.named_scope("wait_three"):
-        arrived = recv3.at[:, pl.ds(0, FIRST)]
+        arrived = recv3.at[pl.ds(0, kept - wide // 2), pl.ds(0, FIRST)]
         pltpu.make_async_copy(arrived, arrived, recv_sems.at[1]).wait()
         loads[6].wait()
+        loads[7].wait()
+    def line_table(odd):
+        for n in range(2):
+            cosine, sine = second_out[n, 0, odd], second_out[n, 1, odd]
+            yield jnp.concatenate(
+                [jnp.concatenate([cosine, -sine], 1), jnp.concatenate([sine, cosine], 1)], 0
+            )
+
+    line_tables = [tuple(line_table(odd)) for odd in range(2)]
+
     with jax.named_scope("inv_0"):
-        lines[...] = to_lines(0)
+        (lines[...],) = to_lines([(0, 0)])
         keep = pl.ds(pl.multiple_of(core * part, SUB), part)
         give_away = pl.ds(pl.multiple_of((1 - core) * part, SUB), part)
         swap = pltpu.make_async_remote_copy(
@@ -323,10 +427,11 @@
         swap.wait()
         shared = list(triple_sums(own, to_field(other_lines[...])))
     with jax.named_scope("wait_four"):
-        arrived = recv3.at[:, pl.ds(FIRST, REST)]
+        arrived = recv3.at[pl.ds(0, kept - wide // 2), pl.ds(0, REST)]
         pltpu.make_async_copy(arrived, arrived, recv_sems.at[4]).wait()
     with jax.named_scope("inv_1"):
-        whole = list(triple_sums(to_field(to_lines(FIRST)), to_field(to_lines(FIRST + 2))))
+        fields = [to_field(values) for values in to_lines([(FIRST, FIRST), (FIRST + 2, FIRST + 1)])]
+        whole = list(triple_sums(*fields))
         lane = lax.broadcasted_iota(jnp.int32, (1, LANES), 1)
         packed = jnp.zeros((1, LANES), jnp.float32)
         for n in range(4):
@@ -376,13 +481,27 @@
     out_ref[...] = out
 
     for n, piece in (
-        (0, send1.at[pl.ds(0, 192)]),
-        (1, send1.at[pl.ds(0, 126)]),
-        (2, send3.at[pl.ds(0, devices - 1), pl.ds(0, FIRST + REST)]),
+        (0, send1.at[pl.ds(0, 3 * 64 - 3 * size // 2)]),
         (3, recv4.at[pl.ds(0, 15)]),
         (4, recv4.at[pl.ds(0, 15)]),
     ):
         pltpu.make_async_copy(piece, piece, send_sems.at[n]).wait()
+
+    @pl.when(jnp.logical_not(edge))
+    def _():
+        for n, piece in (
+            (1, send1.at[pl.ds(0, 2 * (7 * size - 1) + size)]),
+            (2, send3.at[pl.ds(0, devices - 1), pl.ds(0, FIRST + REST)]),
+        ):
+            pltpu.make_async_copy(piece, piece, send_sems.at[n]).wait()
+
+    @pl.when(edge)
+    def _():
+        for n, piece in (
+            (1, send1.at[pl.ds(0, 2 * 7 * size + size - 1)]),
+            (2, send3.at[pl.ds(0, devices - 1), pl.ds(0, (FIRST + REST) // 2)]),
+        ):
+            pltpu.make_async_copy(piece, piece, send_sems.at[n]).wait()
 
 
 def shards(density, shell_edges, triangles):
@@ -394,27 +513,27 @@
     hbm = pl.BlockSpec(memory_space=pl.ANY)
     tiles = pltpu.VMEM((devices, SUB, LANES), jnp.float32)
     pairs = pltpu.VMEM((2, 64, SUB, LANES), jnp.float32)
+    line = pltpu.VMEM((length, LANES), jnp.float32)
     row = pltpu.VMEM((1, 1, LANES), jnp.float32)
     sixteen = pltpu.VMEM((16, 1, LANES), jnp.float32)
     dma = pltpu.SemaphoreType.DMA
     out = pl.pallas_call(
         kernel,
-        out_shape=jax.ShapeDtypeStruct((1, triangles.shape[0]), jnp.float32),
-        in_specs=[pl.BlockSpec(memory_space=pltpu.SMEM), vmem] + [hbm] * 5,
+        out_shape=pltpu.VMEM((1, triangles.shape[0]), jnp.float32),
+        in_specs=[pl.BlockSpec(memory_space=pltpu.SMEM), vmem] + [hbm] * 7,
         out_specs=vmem,
         scratch_shapes=[
             pltpu.VMEM(density.shape, jnp.float32),
             pltpu.VMEM((planes, 2, half, 2 * LANES), jnp.bfloat16),
-            pltpu.VMEM((2, 2, kept, half), jnp.bfloat16),
         ]
         + [pltpu.VMEM(t.shape, jnp.bfloat16) for t in made]
-        + [tiles, tiles, pairs, pairs, tiles, tiles]
+        + [tiles, tiles, pairs, pairs, line, line, tiles, tiles]
         + [
             pltpu.VMEM((coarse, 2 * LANES), jnp.float32),
             pltpu.VMEM((coarse // 2, 2 * LANES), jnp.float32),
         ]
         + [row, sixteen, row, sixteen]
-        + [dma((7,)), dma((5,)), dma((CHUNKS,)), dma((5,)), dma((2,))],
+        + [dma((8,)), dma((5,)), dma((CHUNKS,)), dma((5,)), dma((2,))],
         compiler_params=pltpu.CompilerParams(
             collective_id=0, has_side_effects=True, vmem_limit_bytes=60 << 20
         ),

time: 65 us -> 60.8 us (0.935)
  Pallas kernels: 63.7 us -> 60.2 us
  other arithmetic: 1.19 us -> 0.51 us
    pallas_call x1, Pallas kernels: 63.7 us -> 60.2 us  [shards(): pl.pallas_call(kernel, out_shape=pltpu.VMEM((1, triangles.shape[0]), jnp....]
    mul x1, other arithmetic: 1.19 us -> 0.51 us  [shards(): return out.reshape(-1) * (1.0 / float(coarse) ** 3)]
where the time goes in v4:
time: 60.8 us; the launch traced here: 60.7 us
  Pallas kernels  60.2 us (99%)
    pallas_call x1, Pallas kernels, shards(): pl.pallas_call(kernel, out_shape=pltpu.VMEM((1, triangles.shape[0]), jnp....  60.2 us

profile of v4, /device:TPU:1, one launch (start us, length us, event | category | flops | bytes accessed | tf_op | source)
XLA Modules:
  0.0 60.7 jit_solution(8082746713673663213)
XLA Ops:
  0.0 60.2 %shard_map.91 = f32[1,64]{1,0:T(1,128)S(1)} custom-call(s32[3]{0:T(128)} %edges.1, s32[3,64]{1,0:T(4,128)} %bitcast.3, f32[4,256,512]{2,1,0:T(8,128)} %density.1, bf16[2,512,256]{2,1,0:T(8,128)(2,1)} %constant.14.clone.depth_in_hbm, bf16[2,2,256,256]{3,2,1,0:T(8,128)(2,1)} %constant.15.clone.second_in_hbm, ...), custom_call_target="tpu_custom_call" | custom-call | tf_op jit(solution)/shard_map/pallas_call | solution.py:520
  60.2 0.5 multiply_bitcast_fusion

commit v5 on v4

--- a/solution.py
+++ b/solution.py
@@ -12,7 +12,8 @@
 LANES = 128
 SUB = 8
 FAR_FIRST = (4, 5, 3, 6, 2, 7, 1, 0)
-CHUNKS = 8
+CHUNKS = 16
+EDGE_CHUNKS = 2
 FIRST, REST = 2, 4
 
 
@@ -93,9 +94,9 @@
 
 
 def kernel(
-    edges, triangles, density, depth_in_hbm, second_in_hbm, first_in_hbm, first_out_hbm, second_out_hbm, depth_out_hbm,
+    edges_hbm, triangles_hbm, density, depth_in_hbm, second_in_hbm, first_in_hbm, first_out_hbm, second_out_hbm, depth_out_hbm,
     out_ref,
-    x_ref, modes, depth_in, second_in, first_in, first_out, second_out, depth_out,
+    edges, triangles, x_ref, modes, depth_in, second_in, first_in, first_out, second_out, depth_out,
     send1, recv1, send2, recv2, line_real, line_imag, send3, recv3, lines, other_lines, send4, recv4, send5, recv5,
     load_sems, send_sems, chunk_sems, recv_sems, line_sems,
 ):
@@ -108,9 +109,10 @@
     column = lax.div(slab, 2)
     y_low = lax.div(slab, 64)
     chip = 64 * grp + column
-    mine_j = 4 * core + lax.rem(x + 8 - z, 4)
-    slot = 32 * mine_j + 8 * y + z
-    edge = mine_j == CHUNKS - 1
+    column_z = lax.div(z, 2)
+    mine_j = 8 * core + 4 * lax.rem(z, 2) + lax.rem(x + 4 - column_z, 4)
+    slot = 16 * mine_j + 4 * y + column_z
+    edge = mine_j >= CHUNKS - EDGE_CHUNKS
     landing = lax.rem(slot, 2) * 128 + lax.div(slot, 2)
     planes, half, length = x_ref.shape
     kept = second_in.shape[2]
@@ -126,6 +128,8 @@
         (first_out_hbm, first_out),
         (second_out_hbm, second_out),
         (depth_out_hbm, depth_out),
+        (edges_hbm, edges),
+        (triangles_hbm, triangles),
     ]
     loads = [pltpu.make_async_copy(a, b, load_sems.at[n]) for n, (a, b) in enumerate(copies)]
     for load in loads[:4]:
@@ -161,6 +165,7 @@
     rows = send1.reshape(devices * SUB, LANES)
     size = 64 // CHUNKS
     wide = 4 * size
+    narrow = EDGE_CHUNKS * wide
     for h in range(2):
         with jax.named_scope(f"fwd_{h}"):
             part = kept // 2
@@ -170,18 +175,18 @@
                 c, s = out[:part], out[part:]
                 real, imag = c[:, :LANES] + s[:, LANES:], c[:, LANES:] - s[:, :LANES]
                 start = h * part * SUB + 2 * i
-                full = part - h * wide
+                full = part - h * narrow
                 rows[pl.ds(start, full, stride=SUB), :] = real[:full]
                 rows[pl.ds(start + 1, full, stride=SUB), :] = imag[:full]
                 if h:
-                    rows[pl.ds((kept - wide) * SUB + i, wide, stride=SUB), :] = folded(real[full:], imag[full:])
+                    rows[pl.ds((kept - narrow) * SUB + i, narrow, stride=SUB), :] = folded(real[full:], imag[full:])
         if h == 0:
             for load in loads[4:]:
                 load.start()
             with jax.named_scope("bar"):
                 pl.semaphore_wait(barrier, 66)
         for j in range(h * CHUNKS // 2, (h + 1) * CHUNKS // 2):
-            used = pl.ds(0, SUB if j < CHUNKS - 1 else SUB // 2)
+            used = pl.ds(0, SUB if j < CHUNKS - EDGE_CHUNKS else SUB // 2)
             target = recv1.at[pl.ds(64 * y + size * j, size), used]
             for step in range(1, 4):
                 other = lax.rem(y + step, 4)
@@ -198,7 +203,7 @@
             ).start()
 
     for j in range(CHUNKS):
-        height = SUB if j < CHUNKS - 1 else SUB // 2
+        height = SUB if j < CHUNKS - EDGE_CHUNKS else SUB // 2
         used = pl.ds(0, height)
         with jax.named_scope(f"ring_{j}"):
             everything = recv1.at[pl.ds(0, 4 * size), used]
@@ -211,28 +216,32 @@
                 second = recv1[64 * (low + 2) + size * j : 64 * (low + 2) + size * (j + 1), :height]
                 send2[low, size * j : size * (j + 1), :height] = first + sign * second
 
-            def push(step_z, j=j, used=used):
-                to_z = lax.rem(z + step_z, 8)
+            parity = lax.rem(z + j // 4, 2)
+
+            def push(even_step, odd_step, j=j, used=used, parity=parity):
+                to_z = lax.rem(z + even_step + parity * (odd_step - even_step), 8)
+                to_column = lax.div(to_z, 2)
                 pltpu.make_async_remote_copy(
-                    src_ref=send2.at[:, size * j + to_z, used],
+                    src_ref=send2.at[:, size * j + to_column, used],
                     dst_ref=recv2.at[:, rest, used],
                     send_sem=send_sems.at[1],
                     recv_sem=recv_sems.at[0],
-                    device_id=where_is(y, to_z, lax.rem(to_z + j, 4), j // 4),
+                    device_id=where_is(y, to_z, lax.rem(to_column + j, 4), j // 8),
                     device_id_type=MESH,
                 ).start()
 
-            for step_z in FAR_FIRST[:-1]:
-                push(step_z)
+            push(4, 5)
+            push(6, 3)
+            push(2, 7)
 
             @pl.when(mine_j != j)
             def _(push=push):
-                push(0)
+                push(0, 1)
 
             @pl.when(mine_j == j)
             def _(j=j, used=used):
                 pltpu.make_async_copy(
-                    send2.at[:, size * j + z, used], recv2.at[:, rest, used], recv_sems.at[0]
+                    send2.at[:, size * j + column_z, used], recv2.at[:, rest, used], recv_sems.at[0]
                 ).start()
 
     flat = recv2.reshape(2 * 64 * SUB, LANES)
@@ -253,6 +262,7 @@
                 line_real[pl.ds(low * 64 * planes + i, 64, stride=planes), :] = real
                 line_imag[pl.ds(low * 64 * planes + i, 64, stride=planes), :] = imag
 
+    loads[8].wait()
     radius = [jnp.sqrt(jnp.full((1, LANES), edges[n], jnp.int32).astype(jnp.float32)) for n in range(3)]
     volumes = [4.0 * math.pi / 3.0 * (radius[n + 1] ** 3 - radius[n] ** 3) for n in range(2)]
     with jax.named_scope("mid"):
@@ -364,7 +374,7 @@
     part = coarse // 2
     flat = recv3.reshape(devices * SUB, LANES)
 
-    full = (kept - wide) // 2
+    full = (kept - narrow) // 2
 
     def to_lines(places):
         sums = []
@@ -373,7 +383,7 @@
             columns = []
             for row, edge_row in places:
                 whole = [flat[pl.ds(start + row + k, full, stride=SUB), :] for k in range(2)]
-                ends = unfolded(flat[pl.ds(start + full * SUB + edge_row, wide // 2, stride=SUB), :])
+                ends = unfolded(flat[pl.ds(start + full * SUB + edge_row, narrow // 2, stride=SUB), :])
                 columns.append(jnp.concatenate([whole[0], ends[0], whole[1], ends[1]], 0))
             sums.append(dot(line_tables[odd], split(jnp.concatenate(columns, 1))))
         upper, lower = sums[0] + sums[1], sums[0] - sums[1]
@@ -397,7 +407,7 @@
             yield sum(folded[:, k : k + LANES] for k in range(0, coarse, LANES))
 
     with jax.named_scope("wait_three"):
-        arrived = recv3.at[pl.ds(0, kept - wide // 2), pl.ds(0, FIRST)]
+        arrived = recv3.at[pl.ds(0, kept - narrow // 2), pl.ds(0, FIRST)]
         pltpu.make_async_copy(arrived, arrived, recv_sems.at[1]).wait()
         loads[6].wait()
         loads[7].wait()
@@ -427,7 +437,7 @@
         swap.wait()
         shared = list(triple_sums(own, to_field(other_lines[...])))
     with jax.named_scope("wait_four"):
-        arrived = recv3.at[pl.ds(0, kept - wide // 2), pl.ds(0, REST)]
+        arrived = recv3.at[pl.ds(0, kept - narrow // 2), pl.ds(0, REST)]
         pltpu.make_async_copy(arrived, arrived, recv_sems.at[4]).wait()
     with jax.named_scope("inv_1"):
         fields = [to_field(values) for values in to_lines([(FIRST, FIRST), (FIRST + 2, FIRST + 1)])]
@@ -472,6 +482,7 @@
     with jax.named_scope("sum_two"):
         packed = gather(packed, send5, recv5, 4, 2 * z + core, lambda g: where_is(y, lax.div(g, 2), x, lax.rem(g, 2)))
 
+    loads[9].wait()
     ones = triangles[0:1] + triangles[1:2] + triangles[2:3]
     count = ones.shape[1]
     out = jnp.zeros(ones.shape, jnp.float32)
@@ -481,7 +492,7 @@
     out_ref[...] = out
 
     for n, piece in (
-        (0, send1.at[pl.ds(0, 3 * 64 - 3 * size // 2)]),
+        (0, send1.at[pl.ds(0, 3 * 64 - 3 * narrow // 8)]),
         (3, recv4.at[pl.ds(0, 15)]),
         (4, recv4.at[pl.ds(0, 15)]),
     ):
@@ -490,7 +501,7 @@
     @pl.when(jnp.logical_not(edge))
     def _():
         for n, piece in (
-            (1, send1.at[pl.ds(0, 2 * (7 * size - 1) + size)]),
+            (1, send1.at[pl.ds(0, 2 * 64 - narrow // 4 - 2)]),
             (2, send3.at[pl.ds(0, devices - 1), pl.ds(0, FIRST + REST)]),
         ):
             pltpu.make_async_copy(piece, piece, send_sems.at[n]).wait()
@@ -498,7 +509,7 @@
     @pl.when(edge)
     def _():
         for n, piece in (
-            (1, send1.at[pl.ds(0, 2 * 7 * size + size - 1)]),
+            (1, send1.at[pl.ds(0, 2 * 64 - narrow // 4 - 1)]),
             (2, send3.at[pl.ds(0, devices - 1), pl.ds(0, (FIRST + REST) // 2)]),
         ):
             pltpu.make_async_copy(piece, piece, send_sems.at[n]).wait()
@@ -520,9 +531,11 @@
     out = pl.pallas_call(
         kernel,
         out_shape=pltpu.VMEM((1, triangles.shape[0]), jnp.float32),
-        in_specs=[pl.BlockSpec(memory_space=pltpu.SMEM), vmem] + [hbm] * 7,
+        in_specs=[hbm] * 9,
         out_specs=vmem,
         scratch_shapes=[
+            pltpu.SMEM(shell_edges.shape, jnp.int32),
+            pltpu.VMEM(triangles.shape[::-1], jnp.int32),
             pltpu.VMEM(density.shape, jnp.float32),
             pltpu.VMEM((planes, 2, half, 2 * LANES), jnp.bfloat16),
         ]
@@ -533,7 +546,7 @@
             pltpu.VMEM((coarse // 2, 2 * LANES), jnp.float32),
         ]
         + [row, sixteen, row, sixteen]
-        + [dma((8,)), dma((5,)), dma((CHUNKS,)), dma((5,)), dma((2,))],
+        + [dma((10,)), dma((5,)), dma((CHUNKS,)), dma((5,)), dma((2,))],
         compiler_params=pltpu.CompilerParams(
             collective_id=0, has_side_effects=True, vmem_limit_bytes=60 << 20
         ),

time: 60.8 us -> 60 us (0.987)
  Pallas kernels: 60.2 us -> 59.4 us
    pallas_call x1, Pallas kernels: 60.2 us -> 59.4 us  [shards(): pl.pallas_call(kernel, out_shape=pltpu.VMEM((1, triangles.shape[0]), jnp....]
where the time goes in v5:
time: 60 us; the launch traced here: 59.9 us
  Pallas kernels  59.4 us (99%)
    pallas_call x1, Pallas kernels, shards(): pl.pallas_call(kernel, out_shape=pltpu.VMEM((1, triangles.shape[0]), jnp....  59.4 us

profile of v5, /device:TPU:1, one launch (start us, length us, event | category | flops | bytes accessed | tf_op | source)
XLA Modules:
  0.0 59.9 jit_solution(10390045656851424200)
XLA Ops:
  0.0 59.4 %shard_map.91 = f32[1,64]{1,0:T(1,128)S(1)} custom-call(s32[3]{0:T(128)} %edges_hbm.1, s32[3,64]{1,0:T(4,128)} %bitcast.3, f32[4,256,512]{2,1,0:T(8,128)} %density.1, bf16[2,512,256]{2,1,0:T(8,128)(2,1)} %constant.14.clone.depth_in_hbm, bf16[2,2,256,256]{3,2,1,0:T(8,128)(2,1)} %constant.15.clone.second_in_hbm, ...), custom_call_target="tpu_custom_call" | custom-call | tf_op jit(solution)/shard_map/pallas_call | solution.py:531
  59.4 0.5 multiply_bitcast_fusion

commit v6 on v5

--- a/solution.py
+++ b/solution.py
@@ -14,7 +14,7 @@
 FAR_FIRST = (4, 5, 3, 6, 2, 7, 1, 0)
 CHUNKS = 16
 EDGE_CHUNKS = 2
-FIRST, REST = 2, 4
+USED = 4
 
 
 def halves(table):
@@ -97,7 +97,7 @@
     edges_hbm, triangles_hbm, density, depth_in_hbm, second_in_hbm, first_in_hbm, first_out_hbm, second_out_hbm, depth_out_hbm,
     out_ref,
     edges, triangles, x_ref, modes, depth_in, second_in, first_in, first_out, second_out, depth_out,
-    send1, recv1, send2, recv2, line_real, line_imag, send3, recv3, lines, other_lines, send4, recv4, send5, recv5,
+    send1, recv1, send2, recv2, line_real, line_imag, send_third, recv_third, send3, recv3, lines, other_lines, send4, recv4, send5, recv5,
     load_sems, send_sems, chunk_sems, recv_sems, line_sems,
 ):
     slab, grp = lax.axis_index("slab"), lax.axis_index("grp")
@@ -300,15 +300,48 @@
 
     flat = send3.reshape(devices * SUB, LANES)
 
-    def give_all(start, count, recv_n):
-        these = pl.ds(start, count)
-
+    side = lax.rem(slot, 2)
+
+    def give_third(count):
+        def give(place, to_grp):
+            pltpu.make_async_remote_copy(
+                src_ref=send_third.at[to_grp * 64 + place, pl.ds(0, count)],
+                dst_ref=recv_third.at[lax.div(slot, 2), pl.ds(0, count)],
+                send_sem=send_sems.at[5],
+                recv_sem=recv_sems.at[1],
+                device_id=(2 * place + side, to_grp),
+                device_id_type=MESH,
+            ).start()
+
+        for step_z in FAR_FIRST:
+            to_z = lax.rem(z + step_z, 8)
+
+            def give_two(t, carry, to_z=to_z):
+                place = lax.rem(y_low + lax.div(t, 4), 2) * 32 + to_z * 4 + lax.rem(x + t, 4)
+                give(place, 1 - grp)
+                give(place, grp)
+                return carry
+
+            lax.fori_loop(0 if step_z else 1, 8, give_two, 0)
+        give(column, 1 - grp)
+
+        @pl.when(core != side)
+        def _():
+            give(column, grp)
+
+        @pl.when(core == side)
+        def _():
+            pltpu.make_async_copy(
+                send_third.at[chip, pl.ds(0, count)], recv_third.at[lax.div(slot, 2), pl.ds(0, count)], recv_sems.at[1]
+            ).start()
+
+    def give_all(count):
         def give(n, place, to_grp):
             pltpu.make_async_remote_copy(
-                src_ref=send3.at[n * chips + to_grp * 64 + place, these],
-                dst_ref=recv3.at[landing, these],
+                src_ref=send3.at[n * chips + to_grp * 64 + place, pl.ds(0, count)],
+                dst_ref=recv3.at[landing, pl.ds(0, count)],
                 send_sem=send_sems.at[2],
-                recv_sem=recv_sems.at[recv_n],
+                recv_sem=recv_sems.at[4],
                 device_id=(2 * place + n, to_grp),
                 device_id_type=MESH,
             ).start()
@@ -334,41 +367,40 @@
             @pl.when(core == n)
             def _(n=n):
                 pltpu.make_async_copy(
-                    send3.at[n * chips + chip, these], recv3.at[landing, these], recv_sems.at[recv_n]
+                    send3.at[n * chips + chip, pl.ds(0, count)], recv3.at[landing, pl.ds(0, count)], recv_sems.at[4]
                 ).start()
 
     with jax.named_scope("back_0"):
+        third = send_third.reshape(chips * SUB, LANES)
         a, b, c, d = planes_back(2 * chips, chips)
-        for n, (real, imag) in enumerate(((a, b), (c, d))):
-            start = n * chips * SUB
-            flat[pl.ds(start, chips, stride=SUB), :] = jnp.where(edge, folded(real, imag), real)
-            flat[pl.ds(start + 1, chips, stride=SUB), :] = imag
+        pieces = (jnp.where(edge, folded(a, b), a), jnp.where(edge, folded(c, d), b), c, d)
+        for k, piece in enumerate(pieces):
+            third[pl.ds(k, chips, stride=SUB), :] = piece
     with jax.named_scope("send_0"):
 
         @pl.when(jnp.logical_not(edge))
         def _():
-            give_all(0, FIRST, 1)
+            give_third(USED)
 
         @pl.when(edge)
         def _():
-            give_all(0, FIRST // 2, 1)
+            give_third(USED // 2)
 
     with jax.named_scope("back_1"):
         a, b, c, d = planes_back(0, 2 * chips)
         pieces = (jnp.where(edge, folded(a, b), a), jnp.where(edge, folded(c, d), b), c, d)
         for k, piece in enumerate(pieces):
             for n in range(2):
-                start = n * chips * SUB + FIRST + k
-                flat[pl.ds(start, chips, stride=SUB), :] = piece[n * chips : (n + 1) * chips]
+                flat[pl.ds(n * chips * SUB + k, chips, stride=SUB), :] = piece[n * chips : (n + 1) * chips]
     with jax.named_scope("send_1"):
 
         @pl.when(jnp.logical_not(edge))
         def _():
-            give_all(FIRST, REST, 4)
+            give_all(USED)
 
         @pl.when(edge)
         def _():
-            give_all(FIRST, REST // 2, 4)
+            give_all(USED // 2)
 
     coarse = first_out.shape[2]
     part = coarse // 2
@@ -376,26 +408,17 @@
 
     full = (kept - narrow) // 2
 
-    def to_lines(places):
-        sums = []
-        for odd in range(2):
-            start = odd * chips * SUB
-            columns = []
-            for row, edge_row in places:
-                whole = [flat[pl.ds(start + row + k, full, stride=SUB), :] for k in range(2)]
-                ends = unfolded(flat[pl.ds(start + full * SUB + edge_row, narrow // 2, stride=SUB), :])
-                columns.append(jnp.concatenate([whole[0], ends[0], whole[1], ends[1]], 0))
-            sums.append(dot(line_tables[odd], split(jnp.concatenate(columns, 1))))
-        upper, lower = sums[0] + sums[1], sums[0] - sums[1]
-        for n in range(len(places)):
-            these = slice(n * LANES, (n + 1) * LANES)
-            yield jnp.concatenate(
-                [
-                    jnp.concatenate([upper[:part, these], upper[part:, these]], 1),
-                    jnp.concatenate([lower[:part, these], lower[part:, these]], 1),
-                ],
-                0,
-            )
+    def modes_of(ref, start):
+        columns = []
+        for n in range(2):
+            whole = [ref[pl.ds(start + 2 * n + k, full, stride=SUB), :] for k in range(2)]
+            ends = unfolded(ref[pl.ds(start + full * SUB + n, narrow // 2, stride=SUB), :])
+            columns.append(jnp.concatenate([whole[0], ends[0], whole[1], ends[1]], 0))
+        return split(jnp.concatenate(columns, 1))
+
+    def line(values, n):
+        these = slice(n * LANES, (n + 1) * LANES)
+        return jnp.concatenate([values[:part, these], values[part:, these]], 1)
 
     def to_field(values):
         return dot(split(values), (depth_out[0], depth_out[1]))
@@ -407,10 +430,11 @@
             yield sum(folded[:, k : k + LANES] for k in range(0, coarse, LANES))
 
     with jax.named_scope("wait_three"):
-        arrived = recv3.at[pl.ds(0, kept - narrow // 2), pl.ds(0, FIRST)]
+        arrived = recv_third.at[pl.ds(0, chips - narrow // 4), pl.ds(0, USED)]
         pltpu.make_async_copy(arrived, arrived, recv_sems.at[1]).wait()
         loads[6].wait()
         loads[7].wait()
+
     def line_table(odd):
         for n in range(2):
             cosine, sine = second_out[n, 0, odd], second_out[n, 1, odd]
@@ -418,14 +442,10 @@
                 [jnp.concatenate([cosine, -sine], 1), jnp.concatenate([sine, cosine], 1)], 0
             )
 
-    line_tables = [tuple(line_table(odd)) for odd in range(2)]
-
     with jax.named_scope("inv_0"):
-        (lines[...],) = to_lines([(0, 0)])
-        keep = pl.ds(pl.multiple_of(core * part, SUB), part)
-        give_away = pl.ds(pl.multiple_of((1 - core) * part, SUB), part)
+        lines[...] = dot(tuple(line_table(core)), modes_of(recv_third.reshape(chips * SUB, LANES), 0))
         swap = pltpu.make_async_remote_copy(
-            src_ref=lines.at[give_away],
+            src_ref=lines,
             dst_ref=other_lines,
             send_sem=line_sems.at[0],
             recv_sem=line_sems.at[1],
@@ -433,19 +453,21 @@
             device_id_type=MESH,
         )
         swap.start()
-        own = to_field(lines[keep])
         swap.wait()
-        shared = list(triple_sums(own, to_field(other_lines[...])))
+        mixed = other_lines[...] + jnp.where(core == 0, 1.0, -1.0) * lines[...]
+        shared = list(triple_sums(to_field(line(mixed, 0)), to_field(line(mixed, 1))))
     with jax.named_scope("wait_four"):
-        arrived = recv3.at[pl.ds(0, kept - narrow // 2), pl.ds(0, REST)]
+        arrived = recv3.at[pl.ds(0, kept - narrow // 2), pl.ds(0, USED)]
         pltpu.make_async_copy(arrived, arrived, recv_sems.at[4]).wait()
     with jax.named_scope("inv_1"):
-        fields = [to_field(values) for values in to_lines([(FIRST, FIRST), (FIRST + 2, FIRST + 1)])]
+        sums = [dot(tuple(line_table(odd)), modes_of(flat, odd * chips * SUB)) for odd in range(2)]
+        upper, lower = sums[0] + sums[1], sums[0] - sums[1]
+        fields = [to_field(jnp.concatenate([line(upper, n), line(lower, n)], 0)) for n in range(2)]
         whole = list(triple_sums(*fields))
         lane = lax.broadcasted_iota(jnp.int32, (1, LANES), 1)
         packed = jnp.zeros((1, LANES), jnp.float32)
         for n in range(4):
-            total = whole[n] + jnp.where(core == 0, shared[n], shared[3 - n])
+            total = whole[n] + shared[n]
             packed = jnp.where(lane == n, jnp.sum(total, keepdims=True), packed)
 
     def gather(values, send, recv, n, place, where):
@@ -502,7 +524,8 @@
     def _():
         for n, piece in (
             (1, send1.at[pl.ds(0, 2 * 64 - narrow // 4 - 2)]),
-            (2, send3.at[pl.ds(0, devices - 1), pl.ds(0, FIRST + REST)]),
+            (2, send3.at[pl.ds(0, devices - 1), pl.ds(0, USED)]),
+            (5, send_third.at[pl.ds(0, chips - 1), pl.ds(0, USED)]),
         ):
             pltpu.make_async_copy(piece, piece, send_sems.at[n]).wait()
 
@@ -510,9 +533,17 @@
     def _():
         for n, piece in (
             (1, send1.at[pl.ds(0, 2 * 64 - narrow // 4 - 1)]),
-            (2, send3.at[pl.ds(0, devices - 1), pl.ds(0, (FIRST + REST) // 2)]),
+            (2, send3.at[pl.ds(0, devices - 1), pl.ds(0, USED // 2)]),
+            (5, send_third.at[pl.ds(0, chips - 1), pl.ds(0, USED // 2)]),
         ):
             pltpu.make_async_copy(piece, piece, send_sems.at[n]).wait()
+
+    for alike, count in ((jnp.logical_not(edge), USED), (edge, USED // 2)):
+
+        @pl.when(jnp.logical_and(alike, core != side))
+        def _(count=count):
+            piece = send_third.at[0, pl.ds(0, count)]
+            pltpu.make_async_copy(piece, piece, send_sems.at[5]).wait()
 
 
 def shards(density, shell_edges, triangles):
@@ -525,6 +556,7 @@
     tiles = pltpu.VMEM((devices, SUB, LANES), jnp.float32)
     pairs = pltpu.VMEM((2, 64, SUB, LANES), jnp.float32)
     line = pltpu.VMEM((length, LANES), jnp.float32)
+    thirds = pltpu.VMEM((devices // 2, SUB, LANES), jnp.float32)
     row = pltpu.VMEM((1, 1, LANES), jnp.float32)
     sixteen = pltpu.VMEM((16, 1, LANES), jnp.float32)
     dma = pltpu.SemaphoreType.DMA
@@ -540,13 +572,13 @@
             pltpu.VMEM((planes, 2, half, 2 * LANES), jnp.bfloat16),
         ]
         + [pltpu.VMEM(t.shape, jnp.bfloat16) for t in made]
-        + [tiles, tiles, pairs, pairs, line, line, tiles, tiles]
+        + [tiles, tiles, pairs, pairs, line, line, thirds, thirds, tiles, tiles]
         + [
             pltpu.VMEM((coarse, 2 * LANES), jnp.float32),
-            pltpu.VMEM((coarse // 2, 2 * LANES), jnp.float32),
+            pltpu.VMEM((coarse, 2 * LANES), jnp.float32),
         ]
         + [row, sixteen, row, sixteen]
-        + [dma((10,)), dma((5,)), dma((CHUNKS,)), dma((5,)), dma((2,))],
+        + [dma((10,)), dma((6,)), dma((CHUNKS,)), dma((5,)), dma((2,))],
         compiler_params=pltpu.CompilerParams(
             collective_id=0, has_side_effects=True, vmem_limit_bytes=60 << 20
         ),

time: 60 us -> 60 us (level)
  no operation moved by 1% of the time
where the time goes in v6:
time: 60 us; the launch traced here: 59.9 us
  Pallas kernels  59.4 us (99%)
    pallas_call x1, Pallas kernels, shards(): pl.pallas_call(kernel, out_shape=pltpu.VMEM((1, triangles.shape[0]), jnp....  59.4 us

profile of v6, /device:TPU:1, one launch (start us, length us, event | category | flops | bytes accessed | tf_op | source)
XLA Modules:
  0.0 59.9 jit_solution(11931115483774940123)
XLA Ops:
  0.0 59.4 %shard_map.91 = f32[1,64]{1,0:T(1,128)S(1)} custom-call(s32[3]{0:T(128)} %edges_hbm.1, s32[3,64]{1,0:T(4,128)} %bitcast.3, f32[4,256,512]{2,1,0:T(8,128)} %density.1, bf16[2,512,256]{2,1,0:T(8,128)(2,1)} %constant.14.clone.depth_in_hbm, bf16[2,2,256,256]{3,2,1,0:T(8,128)(2,1)} %constant.15.clone.second_in_hbm, ...), custom_call_target="tpu_custom_call" | custom-call | tf_op jit(solution)/shard_map/pallas_call | solution.py:563
  59.4 0.5 multiply_bitcast_fusion

commit v7 on v6

--- a/solution.py
+++ b/solution.py
@@ -97,7 +97,7 @@
     edges_hbm, triangles_hbm, density, depth_in_hbm, second_in_hbm, first_in_hbm, first_out_hbm, second_out_hbm, depth_out_hbm,
     out_ref,
     edges, triangles, x_ref, modes, depth_in, second_in, first_in, first_out, second_out, depth_out,
-    send1, recv1, send2, recv2, line_real, line_imag, send_third, recv_third, send3, recv3, lines, other_lines, send4, recv4, send5, recv5,
+    send1, recv1, send2, recv2, line_real, line_imag, weights, send_third, recv_third, send3, recv3, lines, other_lines, send4, recv4, send5, recv5,
     load_sems, send_sems, chunk_sems, recv_sems, line_sems,
 ):
     slab, grp = lax.axis_index("slab"), lax.axis_index("grp")
@@ -244,6 +244,19 @@
                     send2.at[:, size * j + column_z, used], recv2.at[:, rest, used], recv_sems.at[0]
                 ).start()
 
+    loads[8].wait()
+    radius = [jnp.sqrt(jnp.full((1, LANES), edges[n], jnp.int32).astype(jnp.float32)) for n in range(3)]
+    volumes = [4.0 * math.pi / 3.0 * (radius[n + 1] ** 3 - radius[n] ** 3) for n in range(2)]
+    shape = (kept, LANES)
+    first = by_parity(lax.broadcasted_iota(jnp.int32, shape, 0), kept, jnp.where)
+    second = signed(slot, kept, jnp.where)
+    third = lax.broadcasted_iota(jnp.int32, shape, 1)
+    squared = first * first + second * second + third * third
+    for n in range(2):
+        scale = lax.rsqrt(float(length) ** 3 * volumes[n])
+        inside = (squared >= edges[n]) & (squared < edges[n + 1])
+        weights[n] = jnp.where(inside, jnp.broadcast_to(scale, shape), 0.0)
+
     flat = recv2.reshape(2 * 64 * SUB, LANES)
 
     @pl.when(jnp.logical_not(edge))
@@ -262,9 +275,6 @@
                 line_real[pl.ds(low * 64 * planes + i, 64, stride=planes), :] = real
                 line_imag[pl.ds(low * 64 * planes + i, 64, stride=planes), :] = imag
 
-    loads[8].wait()
-    radius = [jnp.sqrt(jnp.full((1, LANES), edges[n], jnp.int32).astype(jnp.float32)) for n in range(3)]
-    volumes = [4.0 * math.pi / 3.0 * (radius[n + 1] ** 3 - radius[n] ** 3) for n in range(2)]
     with jax.named_scope("mid"):
         loads[4].wait()
         line = jnp.concatenate([line_real[...], line_imag[...]], 1)
@@ -276,17 +286,9 @@
             real.append(c[:, :LANES] + s[:, LANES:])
             imag.append(c[:, LANES:] - s[:, :LANES])
         real, imag = jnp.concatenate(real, 0), jnp.concatenate(imag, 0)
-        row = lax.broadcasted_iota(jnp.int32, real.shape, 0)
-        first = by_parity(row, kept, jnp.where)
-        second = signed(slot, kept, jnp.where)
-        third = lax.broadcasted_iota(jnp.int32, real.shape, 1)
-        squared = first * first + second * second + third * third
         weighted = []
         for n in range(2):
-            scale = lax.rsqrt(float(length) ** 3 * volumes[n])
-            inside = (squared >= edges[n]) & (squared < edges[n + 1])
-            weight = jnp.where(inside, jnp.broadcast_to(scale, real.shape), 0.0)
-            weighted += [real * weight, imag * weight]
+            weighted += [real * weights[n], imag * weights[n]]
         shells = split(jnp.concatenate(weighted, 1))
         loads[5].wait()
 
@@ -572,7 +574,7 @@
             pltpu.VMEM((planes, 2, half, 2 * LANES), jnp.bfloat16),
         ]
         + [pltpu.VMEM(t.shape, jnp.bfloat16) for t in made]
-        + [tiles, tiles, pairs, pairs, line, line, thirds, thirds, tiles, tiles]
+        + [tiles, tiles, pairs, pairs, line, line, pltpu.VMEM((2, kept, LANES), jnp.float32), thirds, thirds, tiles, tiles]
         + [
             pltpu.VMEM((coarse, 2 * LANES), jnp.float32),
             pltpu.VMEM((coarse, 2 * LANES), jnp.float32),

time: 60 us -> 60 us (level)
  no operation moved by 1% of the time
where the time goes in v7:
time: 60 us; the launch traced here: 59.9 us
  Pallas kernels  59.4 us (99%)
    pallas_call x1, Pallas kernels, shards(): pl.pallas_call(kernel, out_shape=pltpu.VMEM((1, triangles.shape[0]), jnp....  59.4 us

profile of v7, /device:TPU:1, one launch (start us, length us, event | category | flops | bytes accessed | tf_op | source)
XLA Modules:
  0.0 59.9 jit_solution(15815636014449030473)
XLA Ops:
  0.0 59.4 %shard_map.91 = f32[1,64]{1,0:T(1,128)S(1)} custom-call(s32[3]{0:T(128)} %edges_hbm.1, s32[3,64]{1,0:T(4,128)} %bitcast.3, f32[4,256,512]{2,1,0:T(8,128)} %density.1, bf16[2,512,256]{2,1,0:T(8,128)(2,1)} %constant.14.clone.depth_in_hbm, bf16[2,2,256,256]{3,2,1,0:T(8,128)(2,1)} %constant.15.clone.second_in_hbm, ...), custom_call_target="tpu_custom_call" | custom-call | tf_op jit(solution)/shard_map/pallas_call | solution.py:565
  59.4 0.5 multiply_bitcast_fusion
